TPU v7x, 256 devices: a whole 4x4x8 slice. The times are simulated.
256 devices in a mesh: grp: 8 (over x, core), dev: 32 (over z, y).
Axes of the slice: x: 4, y: 4, z: 8, core: 2. Of those that a mesh axis runs over, the one named last changes fastest.
Arguments:
- points: bfloat16 [524288, 1024], P(('grp', 'dev')), may hold values from -6 to 6
- blocks: int32 [524288, 1], P(('grp', 'dev')), may hold values from 0 to 255; in each aligned block of 2048 rows (0 to 2047, 2048 to 4095, ...) at most 16 rows name the same one
- finals: int32 [524288], P(('grp', 'dev')), may hold values from 0 to 255
- centroids: bfloat16 [65536, 1024], P('dev'), may hold values from -6 to 6
Outputs:
- distances: bfloat16 [524288, 256], P(('grp', 'dev'))
- refreshed_centroids: float32 [65536, 1024], P('dev', 'grp')
Inputs may be any that keep to these rules, and one draw needn't show every extreme that they name: `blocks`: among the 2048 rows of one device no block is named by more than 16 rows, and some block by exactly 16. Block b is held by index b // 8 of dev. The point's centroid is row 256 * blocks + finals of centroids.
All inputs are finite; a program needn't handle non-finite values.
Results may differ from a plain program's by a relative error of at most 0.008.
Values may be sent and summed in bfloat16 or wider, within the bound.
A program may use at most 128 MiB of HBM per device.

v0:
```python
import jax
import jax.numpy as jnp
from jax import lax
from jax.sharding import PartitionSpec as P

BS = 256


def block_work(received_points, wanted, centroid_table, width, block_size):
    cent_norm = jnp.sum(jnp.square(centroid_table.astype(jnp.float32)), axis=-1)
    row_norm = jnp.sum(jnp.square(received_points.astype(jnp.float32)), axis=-1)
    cross_products = jnp.einsum(
        "nzy,nvy->nzv", received_points, centroid_table, preferred_element_type=jnp.float32
    )
    dists = ((row_norm[:, :, None] - 2.0 * cross_products + cent_norm[:, None, :]) / width).astype(
        jnp.bfloat16
    )
    onehot_assign = wanted[:, :, None] == jnp.arange(block_size, dtype=jnp.int32)[None, None, :]
    sums = jnp.einsum(
        "xnt,xni->xti",
        onehot_assign.astype(jnp.bfloat16),
        received_points,
        preferred_element_type=jnp.float32,
    )
    counts = jnp.sum(onehot_assign.astype(jnp.float32), axis=1)
    return (dists, sums, counts)


def shards(points, blocks, finals, centroids):
    shard_counts = lax.axis_size("dev")
    count_grp = lax.axis_size("grp")
    npoints, width = points.shape
    block_size = BS
    owned = centroids.shape[0] // block_size
    nblocks = owned * shard_counts
    depth = 2 * npoints // nblocks
    block_ids = blocks[:, 0]
    labels = jnp.arange(nblocks, dtype=jnp.int32)
    member = block_ids[:, None] == labels[None, :]
    lower = (jnp.arange(npoints)[:, None] > jnp.arange(npoints)[None, :]).astype(jnp.bfloat16)
    before = jnp.dot(lower, member.astype(jnp.bfloat16), preferred_element_type=jnp.float32)
    ranks = jnp.sum(jnp.where(member, before, 0.0), axis=1).astype(jnp.int32)
    slots = block_ids * depth + ranks
    outgoing = jnp.zeros((nblocks * depth, width), jnp.bfloat16).at[slots].set(points)
    targets = jnp.full((nblocks * depth,), -1, jnp.int32).at[slots].set(finals)
    outgoing = outgoing.reshape(nblocks, depth, width)
    targets = targets.reshape(nblocks, depth)
    received_points, wanted = (
        lax.all_to_all(outgoing, "dev", split_axis=0, concat_axis=1, tiled=True),
        lax.all_to_all(targets, "dev", split_axis=0, concat_axis=1, tiled=True),
    )
    centroid_table = centroids.reshape(owned, block_size, width)
    dists, sums, counts = block_work(received_points, wanted, centroid_table, width, block_size)
    sums = sums.reshape(owned * block_size, width)
    counts = counts.reshape(owned * block_size)
    returned = lax.all_to_all(dists, "dev", split_axis=1, concat_axis=0, tiled=True)
    distances = returned.reshape(nblocks * depth, block_size)[slots]
    part_sums, part_counts = (
        lax.psum_scatter(sums.astype(jnp.bfloat16), "grp", scatter_dimension=0, tiled=True).astype(
            jnp.float32
        ),
        lax.psum_scatter(
            counts.astype(jnp.bfloat16), "grp", scatter_dimension=0, tiled=True
        ).astype(jnp.float32),
    )
    rows_here = sums.shape[0] // count_grp
    own_rows = lax.dynamic_slice_in_dim(
        centroids, lax.axis_index("grp") * rows_here, rows_here, 0
    ).astype(jnp.float32)
    fresh = (part_sums + own_rows) / (part_counts + 1.0)[:, None]
    refreshed_centroids = lax.all_to_all(
        fresh.astype(jnp.bfloat16), "grp", split_axis=1, concat_axis=0, tiled=True
    ).astype(fresh.dtype)
    return (distances, refreshed_centroids)


def solution(mesh):
    placed = (P(("grp", "dev"), None), P(("grp", "dev"), None), P(("grp", "dev")), P("dev", None))
    return jax.shard_map(
        shards,
        mesh=mesh,
        in_specs=placed,
        out_specs=(P(("grp", "dev"), None), P("dev", "grp")),
        check_vma=False,
    )
```

profile of v0, /device:TPU:6, one launch (start us, length us, event | category | flops | bytes accessed | tf_op | source)
XLA Modules:
  0.0 361.5 jit_solution(12675726830021079699)
XLA Ops:
  7.2 3.2 fusion.7
  10.4 8.2 %scatter_custom_fusion.1 = s32[4096]{0:T(1024)S(1)} fusion(s32[2048]{0:T(1024)S(1)} %bitcast.40, s32[2048]{0:T(1024)} %param.6, s32[]{:T(128)} %constant.9.clone.1), kind=kCustom, calls=%fused_computation.23 | custom fusion | bytes 16896 | tf_op jit(solution)/shard_map/scatter | solution.py:45
  18.8 0.7 reshape.78
  19.5 11.5 %all-to-all-start.2 = ((s32[32,1,128]{2,1,0:T(1,128)}), s32[32,1,128]{2,1,0:T(1,128)S(1)}, u32[]{:S(2)}, u32[]{:S(2)}) async-start(s32[32,1,128]{2,1,0:T(1,128)} %reshape.78), calls=%async_computation.2 | async-start | bytes 32768 | tf_op jit(solution)/shard_map/all_to_all | solution.py:50
  31.0 15.2 %scatter_custom_fusion = bf16[4096,1024]{1,0:T(8,128)(2,1)} fusion(s32[2048]{0:T(1024)S(1)} %bitcast.41, bf16[2048,1024]{1,0:T(8,128)(2,1)} %param.4, bf16[]{:T(256)} %constant.13.clone.1), kind=kCustom, calls=%fused_computation.11 | custom fusion | bytes 8389120 | tf_op jit(solution)/shard_map/scatter | solution.py:44
  46.2 9.9 %all-to-all-start = ((bf16[256,16,1024]{2,1,0:T(8,128)(2,1)}), bf16[256,16,1024]{2,1,0:T(8,128)(2,1)}, u32[]{:S(2)}, u32[]{:S(2)}) async-start(bf16[256,16,1024]{2,1,0:T(8,128)(2,1)} %bitcast.32), calls=%async_computation | async-start | bytes 16777216 | tf_op jit(solution)/shard_map/all_to_all | solution.py:49
  56.4 0.5 broadcast.19
  56.9 0.7 reduce.2
  57.8 189.1 %all-to-all-done = bf16[256,16,1024]{2,1,0:T(8,128)(2,1)} async-done(((bf16[256,16,1024]{2,1,0:T(8,128)(2,1)}), bf16[256,16,1024]{2,1,0:T(8,128)(2,1)}, u32[]{:S(2)}, u32[]{:S(2)}) %all-to-all-start) | async-done | bytes 8388640 | tf_op jit(solution)/shard_map/all_to_all | solution.py:49
  246.9 8.5 %copy.13 = bf16[8,32,16,1024]{3,2,1,0:T(8,128)(2,1)} copy(bf16[8,32,16,1024]{3,2,0,1:T(8,128)(2,1)} %bitcast.5) | data formatting | bytes 16777216 | tf_op jit(solution)/shard_map/all_to_all | solution.py:49
  255.4 7.7 %fusion.5 = bf16[8,256,1024]{2,1,0:T(8,128)(2,1)} fusion(bf16[8,512,1024]{2,1,0:T(8,128)(2,1)} %bitcast.33, s32[8,512]{1,0:T(8,128)S(1)} %eq.34), kind=kOutput, calls=%fused_computation.14 | convolution fusion | flops 2150629376 | bytes 12599296 | tf_op jit(solution)/shard_map/xnt,xni->xti/dot_general | solution.py:19
  263.1 3.1 multiply_reduce_fusion.1
  266.2 5.1 %multiply_reduce_fusion = f32[8,32,16]{2,0,1:T(8,128)S(1)} fusion(bf16[8,32,16,1024]{3,2,0,1:T(8,128)(2,1)} %bitcast.5), kind=kLoop, calls=%fused_computation.3 | loop fusion | flops 12578816 | bytes 8404992 | tf_op jit(solution)/shard_map/reduce_sum | solution.py:11
  271.4 7.5 %multiply_convert_fusion = bf16[8,512,256]{2,1,0:T(8,128)(2,1)S(1)} fusion(bf16[8,512,1024]{2,1,0:T(8,128)(2,1)} %bitcast.34, bf16[8,256,1024]{2,1,0:T(8,128)(2,1)} %bitcast.36, f32[8,256]{1,0:T(8,128)S(1)} %add.38, f32[8,512]{1,0:T(8,128)S(1)} %sub.10), kind=kOutput, calls=%fused_computation.10 | convolution fusion | flops 2152726528 | bytes 14704640 | tf_op jit(solution)/shard_map/nzy,nvy->nzv/dot_general | solution.py:12
  279.0 2.5 copy.14
  281.5 6.8 %all-to-all-start.1 = ((bf16[8,512,256]{2,0,1:T(8,128)(2,1)}), bf16[8,512,256]{2,0,1:T(8,128)(2,1)S(1)}, u32[]{:S(2)}, u32[]{:S(2)}) async-start(bf16[8,512,256]{2,0,1:T(8,128)(2,1)} %copy.14), calls=%async_computation.1 | async-start | bytes 4194304 | tf_op jit(solution)/shard_map/all_to_all | solution.py:56
  288.3 0.6 dynamic-slice
  290.1 10.8 %all-reduce = bf16[2048]{0:T(1024)(128)(2,1)S(1)} all-reduce(bf16[2048]{0:T(1024)(128)(2,1)S(1)} %bitcast.45), channel_id=3, replica_groups=mesh['grp'=8,'dev'=32] {'grp'}, use_global_device_ids=true, to_apply=%region_7.8.clone | all-reduce | flops 2048 | bytes 8192
  301.0 2.2 copy_bitcast_fusion
  303.2 34.4 %all-to-all-done.1 = bf16[8,512,256]{2,0,1:T(8,128)(2,1)S(1)} async-done(((bf16[8,512,256]{2,0,1:T(8,128)(2,1)}), bf16[8,512,256]{2,0,1:T(8,128)(2,1)S(1)}, u32[]{:S(2)}, u32[]{:S(2)}) %all-to-all-start.1) | async-done | bytes 2097184 | tf_op jit(solution)/shard_map/all_to_all | solution.py:56
  337.6 4.7 %all-to-all-start.3 = ((bf16[256,8,128]{2,0,1:T(8,128)(2,1)}), bf16[256,8,128]{2,0,1:T(8,128)(2,1)S(1)}, u32[]{:S(2)}, u32[]{:S(2)}) async-start(bf16[256,8,128]{2,0,1:T(8,128)(2,1)} %copy_bitcast_fusion), calls=%async_computation.4 | async-start | bytes 1048576 | tf_op jit(solution)/shard_map/all_to_all | solution.py:71
  342.3 2.2 copy.15
  344.6 9.1 %gather_fusion = bf16[2048,256]{1,0:T(8,128)(2,1)} fusion(bf16[4096,256]{1,0:T(8,128)(2,1)S(1)} %bitcast.31, s32[2048]{0:T(1024)S(1)} %broadcast_clamp_fusion), kind=kCustom, calls=%fused_computation | custom fusion | bytes 2105344 | tf_op jit(solution)/shard_map/gather | solution.py:57
  353.6 1.0 convert_element_type.81
  (24 shorter events, 1.3 us)
Async XLA Ops:
  7.2 3.2 copy-start.1
  19.5 26.7 %all-to-all-start.2 = ((s32[32,1,128]{2,1,0:T(1,128)}), s32[32,1,128]{2,1,0:T(1,128)S(1)}, u32[]{:S(2)}, u32[]{:S(2)}) async-start(s32[32,1,128]{2,1,0:T(1,128)} %reshape.78), calls=%async_computation.2 | async-start | bytes 32768 | tf_op jit(solution)/shard_map/all_to_all | solution.py:50
  46.2 200.7 %all-to-all-start = ((bf16[256,16,1024]{2,1,0:T(8,128)(2,1)}), bf16[256,16,1024]{2,1,0:T(8,128)(2,1)}, u32[]{:S(2)}, u32[]{:S(2)}) async-start(bf16[256,16,1024]{2,1,0:T(8,128)(2,1)} %bitcast.32), calls=%async_computation | async-start | bytes 16777216 | tf_op jit(solution)/shard_map/all_to_all | solution.py:49
  56.1 244.8 %reduce-scatter.2.cloned.1.call-start = ((), (), s32[]{:S(2)}) async-start(), calls=%async_computation.5 | async-start | bytes 4718592 | tf_op jit(solution)/shard_map/reduce_scatter | solution.py:59
  278.9 9.4 %copy-start.2 = (u32[256]{0:T(256)S(1)}, u32[256]{0:T(256)}, u32[]{:S(2)}) copy-start(u32[256]{0:T(256)} %constant.32) | copy-start | bytes 3076
  281.5 56.1 %all-to-all-start.1 = ((bf16[8,512,256]{2,0,1:T(8,128)(2,1)}), bf16[8,512,256]{2,0,1:T(8,128)(2,1)S(1)}, u32[]{:S(2)}, u32[]{:S(2)}) async-start(bf16[8,512,256]{2,0,1:T(8,128)(2,1)} %copy.14), calls=%async_computation.1 | async-start | bytes 4194304 | tf_op jit(solution)/shard_map/all_to_all | solution.py:56
  337.6 4.7 %copy-start = (bf16[8,512,256]{2,0,1:T(8,128)(2,1)}, bf16[8,512,256]{2,0,1:T(8,128)(2,1)S(1)}, u32[]{:S(2)}) copy-start(bf16[8,512,256]{2,0,1:T(8,128)(2,1)S(1)} %all-to-all-done.1) | copy-start | bytes 6291460
  337.6 16.0 %all-to-all-start.3 = ((bf16[256,8,128]{2,0,1:T(8,128)(2,1)}), bf16[256,8,128]{2,0,1:T(8,128)(2,1)S(1)}, u32[]{:S(2)}, u32[]{:S(2)}) async-start(bf16[256,8,128]{2,0,1:T(8,128)(2,1)} %copy_bitcast_fusion), calls=%async_computation.4 | async-start | bytes 1048576 | tf_op jit(solution)/shard_map/all_to_all | solution.py:71
Sparse Core Ops, SparseCore 0:
  263.2 35.3 reduce-scatter.1
where the time goes:
time: 363 us; the launch traced here: 362 us
  waiting for transfers between devices  224 us (62%)
  local copies, waits for them, and re-layouts  48.1 us (13%)
  starting transfers between devices  33.1 us (9%)
  matrix products  18.4 us (5%)
  between operations  14.9 us (4%)
  other arithmetic  12.7 us (3%)
  blocking collectives  10.8 us (3%)
    all_to_all x1, waiting for transfers between devices, shards(): lax.all_to_all(outgoing, 'dev', split_axis=0, concat_axis=1, tiled=True)  189 us
    all_to_all x1, waiting for transfers between devices, shards(): lax.all_to_all(dists, 'dev', split_axis=1, concat_axis=0, tiled=True)  34.4 us
    scatter x1, local copies, waits for them, and re-layouts, shards(): jnp.zeros((nblocks * depth, width), jnp.bfloat16).at[slots].set(points)  15.2 us
    all_to_all x1, starting transfers between devices, shards(): lax.all_to_all(targets, 'dev', split_axis=0, concat_axis=1, tiled=True)  11.5 us
    unnamed x1, blocking collectives  10.8 us
    all_to_all x1, starting transfers between devices, shards(): lax.all_to_all(outgoing, 'dev', split_axis=0, concat_axis=1, tiled=True)  9.91 us
    gather x1, local copies, waits for them, and re-layouts, shards(): distances = returned.reshape(nblocks * depth, block_size)[slots]  9.06 us
    all_to_all x1, local copies, waits for them, and re-layouts, shards(): lax.all_to_all(outgoing, 'dev', split_axis=0, concat_axis=1, tiled=True)  8.51 us
  transfers between devices with their start and end apart: 5, of which 2 were waited for; matrix products, arithmetic and copies ran while one was open for 14% of the time, Pallas kernels for 0%

commit v1 on v0

v1 whole, which is shorter than its diff:
```python
import jax
import jax.numpy as jnp
from jax import lax
from jax.sharding import Mesh, PartitionSpec as P

BS = 256
NZ = 8
SLAB = ("x", "core", "y")


def shards(points, blocks, finals, centroids):
    npoints, width = points.shape
    owned = centroids.shape[0] // BS
    ny = lax.axis_size("y")
    nblocks = owned * NZ * ny
    depth = 2 * npoints // nblocks
    g = lax.axis_index(("x", "core"))
    own_block = lax.dynamic_slice_in_dim(centroids, g * BS, BS, 0)
    table = lax.all_gather(own_block, "z", axis=0, tiled=False)

    block_ids = blocks[:, 0]
    dest = ((block_ids % owned) * ny + (block_ids // owned) % ny) * NZ + block_ids // (owned * ny)
    labels = jnp.arange(nblocks, dtype=jnp.int32)
    member = dest[:, None] == labels[None, :]
    lower = (jnp.arange(npoints)[:, None] > jnp.arange(npoints)[None, :]).astype(jnp.bfloat16)
    before = jnp.dot(lower, member.astype(jnp.bfloat16), preferred_element_type=jnp.float32)
    ranks = jnp.sum(jnp.where(member, before, 0.0), axis=1).astype(jnp.int32)
    slots = dest * depth + ranks
    outgoing = jnp.zeros((nblocks * depth, width), jnp.bfloat16).at[slots].set(points)
    targets = jnp.full((nblocks * depth,), -1, jnp.int32).at[slots].set(finals)
    outgoing = outgoing.reshape(nblocks, depth, width)
    targets = targets.reshape(nblocks, depth)
    received = lax.all_to_all(outgoing, SLAB, split_axis=0, concat_axis=1, tiled=True)
    wanted = lax.all_to_all(targets, SLAB, split_axis=0, concat_axis=1, tiled=True)

    cent_norm = jnp.sum(jnp.square(table.astype(jnp.float32)), axis=-1)
    row_norm = jnp.sum(jnp.square(received.astype(jnp.float32)), axis=-1)
    cross = jnp.einsum("nzy,nvy->nzv", received, table, preferred_element_type=jnp.float32)
    dists = ((row_norm[:, :, None] - 2.0 * cross + cent_norm[:, None, :]) / width).astype(jnp.bfloat16)
    onehot = wanted[:, :, None] == jnp.arange(BS, dtype=jnp.int32)[None, None, :]
    sums = jnp.einsum("xnt,xni->xti", onehot.astype(jnp.bfloat16), received, preferred_element_type=jnp.float32)
    counts = jnp.sum(onehot.astype(jnp.float32), axis=1)
    returned = lax.all_to_all(dists, SLAB, split_axis=1, concat_axis=0, tiled=True)
    distances = returned.reshape(nblocks * depth, BS)[slots]
    own_sums = lax.psum_scatter(sums.astype(jnp.bfloat16), "z", scatter_dimension=0, tiled=True)
    own_sums = own_sums.reshape(BS, width).astype(jnp.float32)
    own_counts = lax.psum_scatter(counts, "z", scatter_dimension=0, tiled=True).reshape(BS)
    fresh = (own_sums + own_block.astype(jnp.float32)) / (own_counts + 1.0)[:, None]
    refreshed = lax.all_to_all(
        fresh.astype(jnp.bfloat16), ("x", "core"), split_axis=1, concat_axis=0, tiled=True
    ).astype(jnp.float32)
    return distances, refreshed


def solution(mesh):
    ngrp, ndev = mesh.shape["grp"], mesh.shape["dev"]
    fine = Mesh(mesh.devices.reshape(ngrp // 2, 2, NZ, ndev // NZ), ("x", "core", "z", "y"))
    rows = ("x", "core", "z", "y")
    return jax.shard_map(
        shards,
        mesh=fine,
        in_specs=(P(rows, None), P(rows, None), P(rows), P(("z", "y"), None)),
        out_specs=(P(rows, None), P(("z", "y"), ("x", "core"))),
        check_vma=False,
    )
```

time: 363 us -> 355 us (0.978)
  waiting for transfers between devices: 224 us -> 210 us
  blocking collectives: 10.8 us -> 20.9 us
  starting transfers between devices: 33.1 us -> 27.4 us
    all_to_all x4, waiting for transfers between devices: 223 us -> 133 us  [the longest x1 107 us: shards(): lax.all_to_all(outgoing, SLAB, split_axis=0, concat_axis=1, tiled=True)]
    all_gather x0 -> x1, waiting for transfers between devices: none -> 42.5 us  [shards(): table = lax.all_gather(own_block, 'z', axis=0, tiled=False)]
    reduce_scatter x1, waiting for transfers between devices: 0.01 us -> 33.8 us  [shards(): lax.psum_scatter(sums.astype(jnp.bfloat16), 'z', scatter_dimension=0, til...]
    unnamed x1, blocking collectives: 10.8 us -> 20.9 us
    all_to_all x4, starting transfers between devices: 32.9 us -> 27.1 us  [the longest x1 7.61 us: shards(): lax.all_to_all(targets, SLAB, split_axis=0, concat_axis=1, tiled=True)]
    all_to_all x5 -> x6, local copies, waits for them, and re-layouts: 11.4 us -> 12.3 us  [the longest x1 8.51 us: shards(): lax.all_to_all(outgoing, SLAB, split_axis=0, concat_axis=1, tiled=True)]
  transfers between devices with their start and end apart: 5 -> 6, of which waited for: 2 -> 4; matrix products, arithmetic and copies ran while one was open for 14% -> 11% of each run, Pallas kernels for 0% -> 0%
where the time goes in v1:
time: 355 us; the launch traced here: 354 us
  waiting for transfers between devices  210 us (59%)
  local copies, waits for them, and re-layouts  51.2 us (14%)
  starting transfers between devices  27.4 us (8%)
  blocking collectives  20.9 us (6%)
  matrix products  16 us (5%)
  other arithmetic  14.4 us (4%)
  between operations  14.2 us (4%)
    all_to_all x1, waiting for transfers between devices, shards(): lax.all_to_all(outgoing, SLAB, split_axis=0, concat_axis=1, tiled=True)  107 us
    all_gather x1, waiting for transfers between devices, shards(): table = lax.all_gather(own_block, 'z', axis=0, tiled=False)  42.5 us
    reduce_scatter x1, waiting for transfers between devices, shards(): lax.psum_scatter(sums.astype(jnp.bfloat16), 'z', scatter_dimension=0, til...  33.8 us
    all_to_all x1, waiting for transfers between devices, shards(): lax.all_to_all(dists, SLAB, split_axis=1, concat_axis=0, tiled=True)  26 us
    unnamed x1, blocking collectives  20.9 us
    scatter x1, local copies, waits for them, and re-layouts, shards(): jnp.zeros((nblocks * depth, width), jnp.bfloat16).at[slots].set(points)  15.2 us
    gather x1, local copies, waits for them, and re-layouts, shards(): distances = returned.reshape(nblocks * depth, BS)[slots]  9.06 us
    all_to_all x1, local copies, waits for them, and re-layouts, shards(): lax.all_to_all(outgoing, SLAB, split_axis=0, concat_axis=1, tiled=True)  8.51 us
  transfers between devices with their start and end apart: 6, of which 4 were waited for; matrix products, arithmetic and copies ran while one was open for 11% of the time, Pallas kernels for 0%

profile of v1, /device:TPU:6, one launch (start us, length us, event | category | flops | bytes accessed | tf_op | source)
XLA Modules:
  0.0 353.8 jit_solution(4961574564626492864)
XLA Ops:
  8.0 2.4 fusion.7
  10.6 8.2 %scatter_custom_fusion.1 = s32[4096]{0:T(1024)S(1)} fusion(s32[2048]{0:T(1024)S(1)} %bitcast.43, s32[2048]{0:T(1024)} %param.6, s32[]{:T(128)} %constant.71.clone.1), kind=kCustom, calls=%fused_computation.39 | custom fusion | bytes 16896 | tf_op jit(solution)/shard_map/scatter | solution.py:30
  19.6 7.6 %all-to-all-start.2 = ((s32[32,1,128]{2,1,0:T(1,128)}), s32[32,1,128]{2,1,0:T(1,128)S(1)}, u32[]{:S(2)}, u32[]{:S(2)}) async-start(s32[32,1,128]{2,1,0:T(1,128)} %reshape.80), calls=%async_computation.2 | async-start | bytes 32768 | tf_op jit(solution)/shard_map/all_to_all | solution.py:34
  27.2 15.2 %scatter_custom_fusion = bf16[4096,1024]{1,0:T(8,128)(2,1)} fusion(s32[2048]{0:T(1024)S(1)} %bitcast.44, bf16[2048,1024]{1,0:T(8,128)(2,1)} %param.4, bf16[]{:T(256)} %constant.64.clone.1), kind=kCustom, calls=%fused_computation.11 | custom fusion | bytes 8389120 | tf_op jit(solution)/shard_map/scatter | solution.py:29
  42.5 7.4 %all-to-all-start = ((bf16[256,16,1024]{2,1,0:T(8,128)(2,1)}), bf16[256,16,1024]{2,1,0:T(8,128)(2,1)}, u32[]{:S(2)}, u32[]{:S(2)}) async-start(bf16[256,16,1024]{2,1,0:T(8,128)(2,1)} %bitcast.35), calls=%async_computation | async-start | bytes 16777216 | tf_op jit(solution)/shard_map/all_to_all | solution.py:33
  51.6 107.4 %all-to-all-done = bf16[256,16,1024]{2,1,0:T(8,128)(2,1)} async-done(((bf16[256,16,1024]{2,1,0:T(8,128)(2,1)}), bf16[256,16,1024]{2,1,0:T(8,128)(2,1)}, u32[]{:S(2)}, u32[]{:S(2)}) %all-to-all-start) | async-done | bytes 8388640 | tf_op jit(solution)/shard_map/all_to_all | solution.py:33
  159.0 8.5 %copy.13 = bf16[8,32,16,1024]{3,2,1,0:T(8,128)(2,1)} copy(bf16[8,32,16,1024]{3,2,0,1:T(8,128)(2,1)} %bitcast.5) | data formatting | bytes 16777216 | tf_op jit(solution)/shard_map/all_to_all | solution.py:33
  167.5 7.7 %fusion.5 = bf16[8,256,1024]{2,1,0:T(8,128)(2,1)} fusion(bf16[8,512,1024]{2,1,0:T(8,128)(2,1)} %bitcast.36, s32[8,512]{1,0:T(8,128)S(1)} %eq.37), kind=kOutput, calls=%fused_computation.14 | convolution fusion | flops 2150629376 | bytes 12599296 | tf_op jit(solution)/shard_map/xnt,xni->xti/dot_general | solution.py:41
  176.9 20.9 %all-reduce = f32[8,256]{1,0:T(8,128)S(1)} all-reduce(f32[8,256]{1,0:T(8,128)S(1)} %convert_reduce_fusion), channel_id=4, replica_groups=mesh['x'=4,'core'=2,'z'=8,'y'=4] {'z'}, use_global_device_ids=true, to_apply=%region_7.8.clone | all-reduce | flops 2048 | bytes 16384
  198.4 33.8 %reduce-scatter.2.cloned.1.call-done = bf16[1,256,1024]{2,1,0:T(8,128)(2,1)} async-done(((bf16[8,256,1024]{2,1,0:T(8,128)(2,1)}), bf16[1,256,1024]{2,1,0:T(8,128)(2,1)}) %reduce-scatter.2.cloned.1.call-update) | async-done | bytes 524304 | tf_op jit(solution)/shard_map/reduce_scatter | solution.py:45
  232.2 2.3 fusion.11
  234.5 5.1 %multiply_reduce_fusion = f32[8,32,16]{2,0,1:T(8,128)S(1)} fusion(bf16[8,32,16,1024]{3,2,0,1:T(8,128)(2,1)} %bitcast.5), kind=kLoop, calls=%fused_computation.3 | loop fusion | flops 12578816 | bytes 8404992 | tf_op jit(solution)/shard_map/reduce_sum | solution.py:37
  239.8 0.9 copy.20
  240.7 4.6 %all-to-all-start.3 = ((bf16[256,8,128]{2,0,1:T(8,128)(2,1)}), bf16[256,8,128]{2,0,1:T(8,128)(2,1)S(1)}, u32[]{:S(2)}, u32[]{:S(2)}) async-start(bf16[256,8,128]{2,0,1:T(8,128)(2,1)} %bitcast.31), calls=%async_computation.4 | async-start | bytes 1048576 | tf_op jit(solution)/shard_map/all_to_all | solution.py:49
  245.3 42.5 %all-gather.3.cloned.1.call-done = bf16[2048,1024]{1,0:T(8,128)(2,1)} async-done(((bf16[256,1024]{1,0:T(8,128)(2,1)}), bf16[2048,1024]{1,0:T(8,128)(2,1)}) %all-gather.3.cloned.1.call-update) | async-done | bytes 4194320 | tf_op jit(solution)/shard_map/all_gather | solution.py:19
  287.8 3.2 multiply_reduce_fusion.1
  291.3 5.9 %multiply_convert_fusion = bf16[8,512,256]{2,1,0:T(8,128)(2,1)S(1)} fusion(bf16[8,512,1024]{2,1,0:T(8,128)(2,1)} %bitcast.37, bf16[8,256,1024]{2,1,0:T(8,128)(2,1)S(1)} %bitcast.40, f32[8,256]{1,0:T(8,128)S(1)} %multiply_reduce_fusion.1, f32[8,512]{1,0:T(8,128)S(1)} %sub.22), kind=kOutput, calls=%fused_computation.10 | convolution fusion | flops 2152726528 | bytes 14704640 | tf_op jit(solution)/shard_map/nzy,nvy->nzv/dot_general | solution.py:38
  297.2 2.5 copy.14
  299.8 7.5 %all-to-all-start.1 = ((bf16[8,512,256]{2,0,1:T(8,128)(2,1)}), bf16[8,512,256]{2,0,1:T(8,128)(2,1)S(1)}, u32[]{:S(2)}, u32[]{:S(2)}) async-start(bf16[8,512,256]{2,0,1:T(8,128)(2,1)} %copy.14), calls=%async_computation.1 | async-start | bytes 4194304 | tf_op jit(solution)/shard_map/all_to_all | solution.py:43
  307.2 1.0 convert_element_type.69
  308.3 26.0 %all-to-all-done.1 = bf16[8,512,256]{2,0,1:T(8,128)(2,1)S(1)} async-done(((bf16[8,512,256]{2,0,1:T(8,128)(2,1)}), bf16[8,512,256]{2,0,1:T(8,128)(2,1)S(1)}, u32[]{:S(2)}, u32[]{:S(2)}) %all-to-all-start.1) | async-done | bytes 2097184 | tf_op jit(solution)/shard_map/all_to_all | solution.py:43
  334.3 1.3 copy-done
  335.6 2.2 copy.15
  337.9 9.1 %gather_fusion = bf16[2048,256]{1,0:T(8,128)(2,1)} fusion(bf16[4096,256]{1,0:T(8,128)(2,1)S(1)} %bitcast.34, s32[2048]{0:T(1024)S(1)} %broadcast_clamp_fusion), kind=kCustom, calls=%fused_computation | custom fusion | bytes 2105344 | tf_op jit(solution)/shard_map/gather | solution.py:44
  (29 shorter events, 6.2 us)
Async XLA Ops:
  8.0 2.4 copy-start.2
  19.6 22.9 %all-to-all-start.2 = ((s32[32,1,128]{2,1,0:T(1,128)}), s32[32,1,128]{2,1,0:T(1,128)S(1)}, u32[]{:S(2)}, u32[]{:S(2)}) async-start(s32[32,1,128]{2,1,0:T(1,128)} %reshape.80), calls=%async_computation.2 | async-start | bytes 32768 | tf_op jit(solution)/shard_map/all_to_all | solution.py:34
  42.5 116.5 %all-to-all-start = ((bf16[256,16,1024]{2,1,0:T(8,128)(2,1)}), bf16[256,16,1024]{2,1,0:T(8,128)(2,1)}, u32[]{:S(2)}, u32[]{:S(2)}) async-start(bf16[256,16,1024]{2,1,0:T(8,128)(2,1)} %bitcast.35), calls=%async_computation | async-start | bytes 16777216 | tf_op jit(solution)/shard_map/all_to_all | solution.py:33
  49.9 182.3 %reduce-scatter.2.cloned.1.call-start = ((), (), s32[]{:S(2)}) async-start(), calls=%async_computation.5 | async-start | bytes 4718592 | tf_op jit(solution)/shard_map/reduce_scatter | solution.py:45
  175.2 0.7 copy-start.3
  175.2 112.6 %all-gather.3.cloned.1.call-start = ((), (), s32[]{:S(2)}) async-start(), calls=%async_computation.6 | async-start | bytes 4718592 | tf_op jit(solution)/shard_map/all_gather | solution.py:19
  240.7 59.1 %all-to-all-start.3 = ((bf16[256,8,128]{2,0,1:T(8,128)(2,1)}), bf16[256,8,128]{2,0,1:T(8,128)(2,1)S(1)}, u32[]{:S(2)}, u32[]{:S(2)}) async-start(bf16[256,8,128]{2,0,1:T(8,128)(2,1)} %bitcast.31), calls=%async_computation.4 | async-start | bytes 1048576 | tf_op jit(solution)/shard_map/all_to_all | solution.py:49
  287.8 3.4 copy-start.1
  299.8 34.5 %all-to-all-start.1 = ((bf16[8,512,256]{2,0,1:T(8,128)(2,1)}), bf16[8,512,256]{2,0,1:T(8,128)(2,1)S(1)}, u32[]{:S(2)}, u32[]{:S(2)}) async-start(bf16[8,512,256]{2,0,1:T(8,128)(2,1)} %copy.14), calls=%async_computation.1 | async-start | bytes 4194304 | tf_op jit(solution)/shard_map/all_to_all | solution.py:43
  334.3 1.4 copy-start
Sparse Core Ops, SparseCore 0:
  175.3 56.8 reduce-scatter.1
  234.7 53.1 all-gather.2

commit v2 on v1

--- a/solution.py
+++ b/solution.py
@@ -30,6 +30,7 @@
     targets = jnp.full((nblocks * depth,), -1, jnp.int32).at[slots].set(finals)
     outgoing = outgoing.reshape(nblocks, depth, width)
     targets = targets.reshape(nblocks, depth)
+    outgoing, table = lax.optimization_barrier((outgoing, table))
     received = lax.all_to_all(outgoing, SLAB, split_axis=0, concat_axis=1, tiled=True)
     wanted = lax.all_to_all(targets, SLAB, split_axis=0, concat_axis=1, tiled=True)
 

time: 355 us -> 282 us (0.79)
  waiting for transfers between devices: 210 us -> 142 us
  blocking collectives: 20.9 us -> 16.7 us
    all_to_all x1, waiting for transfers between devices: 26 us -> 0.01 us  [shards(): lax.all_to_all(dists, SLAB, split_axis=1, concat_axis=0, tiled=True)]
    reduce_scatter x1, waiting for transfers between devices: 33.8 us -> 10.7 us  [shards(): lax.psum_scatter(sums.astype(jnp.bfloat16), 'z', scatter_dimension=0, til...]
    all_gather x1, waiting for transfers between devices: 42.5 us -> 23.6 us  [shards(): table = lax.all_gather(own_block, 'z', axis=0, tiled=False)]
    unnamed x1, blocking collectives: 20.9 us -> 16.7 us
  transfers between devices with their start and end apart: 6 -> 6, of which waited for: 4 -> 3; matrix products, arithmetic and copies ran while one was open for 11% -> 22% of each run, Pallas kernels for 0% -> 0%
where the time goes in v2:
time: 282 us; the launch traced here: 280 us
  waiting for transfers between devices  142 us (50%)
  local copies, waits for them, and re-layouts  50 us (18%)
  starting transfers between devices  26.2 us (9%)
  matrix products  17.4 us (6%)
  blocking collectives  16.7 us (6%)
  other arithmetic  14.2 us (5%)
  between operations  14.2 us (5%)
    all_to_all x1, waiting for transfers between devices, shards(): lax.all_to_all(outgoing, SLAB, split_axis=0, concat_axis=1, tiled=True)  107 us
    all_gather x1, waiting for transfers between devices, shards(): table = lax.all_gather(own_block, 'z', axis=0, tiled=False)  23.6 us
    unnamed x1, blocking collectives  16.7 us
    scatter x1, local copies, waits for them, and re-layouts, shards(): jnp.zeros((nblocks * depth, width), jnp.bfloat16).at[slots].set(points)  15.3 us
    reduce_scatter x1, waiting for transfers between devices, shards(): lax.psum_scatter(sums.astype(jnp.bfloat16), 'z', scatter_dimension=0, til...  10.7 us
    gather x1, local copies, waits for them, and re-layouts, shards(): distances = returned.reshape(nblocks * depth, BS)[slots]  9.06 us
    all_to_all x1, local copies, waits for them, and re-layouts, shards(): lax.all_to_all(outgoing, SLAB, split_axis=0, concat_axis=1, tiled=True)  8.51 us
    scatter x1, local copies, waits for them, and re-layouts, shards(): targets = jnp.full((nblocks * depth,), -1, jnp.int32).at[slots].set(finals)  8.23 us
  transfers between devices with their start and end apart: 6, of which 3 were waited for; matrix products, arithmetic and copies ran while one was open for 22% of the time, Pallas kernels for 0%

profile of v2, /device:TPU:6, one launch (start us, length us, event | category | flops | bytes accessed | tf_op | source)
XLA Modules:
  0.0 280.4 jit_solution(6789474514913729896)
XLA Ops:
  7.2 1.9 constant_dynamic-slice_fusion
  9.1 0.8 multiply_add_fusion
  9.9 2.4 fusion.7
  12.5 8.2 %scatter_custom_fusion.1 = s32[4096]{0:T(1024)S(1)} fusion(s32[2048]{0:T(1024)S(1)} %bitcast.42, s32[2048]{0:T(1024)} %param.6, s32[]{:T(128)} %constant.71.clone.1), kind=kCustom, calls=%fused_computation.39 | custom fusion | bytes 16896 | tf_op jit(solution)/shard_map/scatter | solution.py:30
  20.9 0.7 reshape.80
  21.6 7.6 %all-to-all-start.2 = ((s32[32,1,128]{2,1,0:T(1,128)}), s32[32,1,128]{2,1,0:T(1,128)S(1)}, u32[]{:S(2)}, u32[]{:S(2)}) async-start(s32[32,1,128]{2,1,0:T(1,128)} %reshape.80), calls=%async_computation.2 | async-start | bytes 32768 | tf_op jit(solution)/shard_map/all_to_all | solution.py:35
  29.2 15.3 %scatter_custom_fusion = bf16[4096,1024]{1,0:T(8,128)(2,1)} fusion(s32[2048]{0:T(1024)S(1)} %bitcast.43, bf16[2048,1024]{1,0:T(8,128)(2,1)} %param.4, bf16[]{:T(256)} %constant.64.clone.1), kind=kCustom, calls=%fused_computation.11 | custom fusion | bytes 8389120 | tf_op jit(solution)/shard_map/scatter | solution.py:29
  44.5 23.6 %all-gather.3.cloned.1.call-done = bf16[2048,1024]{1,0:T(8,128)(2,1)} async-done(((bf16[256,1024]{1,0:T(8,128)(2,1)}), bf16[2048,1024]{1,0:T(8,128)(2,1)}) %all-gather.3.cloned.1.call-update) | async-done | bytes 4194320 | tf_op jit(solution)/shard_map/all_gather | solution.py:19
  68.0 7.5 %all-to-all-start = ((bf16[256,16,1024]{2,1,0:T(8,128)(2,1)}), bf16[256,16,1024]{2,1,0:T(8,128)(2,1)}, u32[]{:S(2)}, u32[]{:S(2)}) async-start(bf16[256,16,1024]{2,1,0:T(8,128)(2,1)} %bitcast.34), calls=%async_computation | async-start | bytes 16777216 | tf_op jit(solution)/shard_map/all_to_all | solution.py:34
  77.2 107.4 %all-to-all-done = bf16[256,16,1024]{2,1,0:T(8,128)(2,1)} async-done(((bf16[256,16,1024]{2,1,0:T(8,128)(2,1)}), bf16[256,16,1024]{2,1,0:T(8,128)(2,1)}, u32[]{:S(2)}, u32[]{:S(2)}) %all-to-all-start) | async-done | bytes 8388640 | tf_op jit(solution)/shard_map/all_to_all | solution.py:34
  184.6 8.5 %copy.13 = bf16[8,32,16,1024]{3,2,1,0:T(8,128)(2,1)} copy(bf16[8,32,16,1024]{3,2,0,1:T(8,128)(2,1)} %bitcast.6) | data formatting | bytes 16777216 | tf_op jit(solution)/shard_map/all_to_all | solution.py:34
  193.1 7.7 %fusion.5 = bf16[8,256,1024]{2,1,0:T(8,128)(2,1)} fusion(bf16[8,512,1024]{2,1,0:T(8,128)(2,1)} %bitcast.35, s32[8,512]{1,0:T(8,128)S(1)} %eq.37), kind=kOutput, calls=%fused_computation.14 | convolution fusion | flops 2150629376 | bytes 12599296 | tf_op jit(solution)/shard_map/xnt,xni->xti/dot_general | solution.py:42
  200.9 3.1 %multiply_reduce_fusion.1 = f32[8,256]{1,0:T(8,128)S(1)} fusion(bf16[8,256,1024]{2,1,0:T(8,128)(2,1)} %bitcast.38), kind=kLoop, calls=%fused_computation.6 | loop fusion | flops 6289408 | bytes 4202496 | tf_op jit(solution)/shard_map/reduce_sum | solution.py:37
  203.9 5.1 %multiply_reduce_fusion = f32[8,32,16]{2,0,1:T(8,128)S(1)} fusion(bf16[8,32,16,1024]{3,2,0,1:T(8,128)(2,1)} %bitcast.6), kind=kLoop, calls=%fused_computation.3 | loop fusion | flops 12578816 | bytes 8404992 | tf_op jit(solution)/shard_map/reduce_sum | solution.py:38
  209.2 7.3 %multiply_convert_fusion = bf16[8,512,256]{2,1,0:T(8,128)(2,1)S(1)} fusion(bf16[8,512,1024]{2,1,0:T(8,128)(2,1)} %bitcast.36, bf16[8,256,1024]{2,1,0:T(8,128)(2,1)} %bitcast.39, f32[8,256]{1,0:T(8,128)S(1)} %multiply_reduce_fusion.1, f32[8,512]{1,0:T(8,128)S(1)} %sub.22), kind=kOutput, calls=%fused_computation.10 | convolution fusion | flops 2152726528 | bytes 14704640 | tf_op jit(solution)/shard_map/nzy,nvy->nzv/dot_general | solution.py:39
  216.5 2.5 copy.14
  219.0 6.0 %all-to-all-start.1 = ((bf16[8,512,256]{2,0,1:T(8,128)(2,1)}), bf16[8,512,256]{2,0,1:T(8,128)(2,1)S(1)}, u32[]{:S(2)}, u32[]{:S(2)}) async-start(bf16[8,512,256]{2,0,1:T(8,128)(2,1)} %copy.14), calls=%async_computation.1 | async-start | bytes 4194304 | tf_op jit(solution)/shard_map/all_to_all | solution.py:44
  226.1 16.7 %all-reduce = f32[8,256]{1,0:T(8,128)S(1)} all-reduce(f32[8,256]{1,0:T(8,128)S(1)} %convert_reduce_fusion), channel_id=4, replica_groups=mesh['x'=4,'core'=2,'z'=8,'y'=4] {'z'}, use_global_device_ids=true, to_apply=%region_7.8.clone | all-reduce | flops 2048 | bytes 16384
  243.5 10.7 %reduce-scatter.2.cloned.1.call-done = bf16[1,256,1024]{2,1,0:T(8,128)(2,1)} async-done(((bf16[8,256,1024]{2,1,0:T(8,128)(2,1)}), bf16[1,256,1024]{2,1,0:T(8,128)(2,1)}) %reduce-scatter.2.cloned.1.call-update) | async-done | bytes 524304 | tf_op jit(solution)/shard_map/reduce_scatter | solution.py:46
  254.2 2.2 copy_bitcast_fusion
  256.4 4.8 %all-to-all-start.3 = ((bf16[256,8,128]{2,0,1:T(8,128)(2,1)}), bf16[256,8,128]{2,0,1:T(8,128)(2,1)S(1)}, u32[]{:S(2)}, u32[]{:S(2)}) async-start(bf16[256,8,128]{2,0,1:T(8,128)(2,1)} %copy_bitcast_fusion), calls=%async_computation.4 | async-start | bytes 1048576 | tf_op jit(solution)/shard_map/all_to_all | solution.py:50
  261.2 2.2 copy.15
  263.5 9.1 %gather_fusion = bf16[2048,256]{1,0:T(8,128)(2,1)} fusion(bf16[4096,256]{1,0:T(8,128)(2,1)S(1)} %bitcast.33, s32[2048]{0:T(1024)S(1)} %broadcast_clamp_fusion), kind=kCustom, calls=%fused_computation | custom fusion | bytes 2105344 | tf_op jit(solution)/shard_map/gather | solution.py:45
  272.5 1.0 convert_element_type.69
  (27 shorter events, 3.8 us)
Async XLA Ops:
  7.2 60.9 %all-gather.3.cloned.1.call-start = ((), (), s32[]{:S(2)}) async-start(), calls=%async_computation.6 | async-start | bytes 4718592 | tf_op jit(solution)/shard_map/all_gather | solution.py:19
  9.9 2.4 copy-start.1
  21.6 46.5 %all-to-all-start.2 = ((s32[32,1,128]{2,1,0:T(1,128)}), s32[32,1,128]{2,1,0:T(1,128)S(1)}, u32[]{:S(2)}, u32[]{:S(2)}) async-start(s32[32,1,128]{2,1,0:T(1,128)} %reshape.80), calls=%async_computation.2 | async-start | bytes 32768 | tf_op jit(solution)/shard_map/all_to_all | solution.py:35
  68.0 116.6 %all-to-all-start = ((bf16[256,16,1024]{2,1,0:T(8,128)(2,1)}), bf16[256,16,1024]{2,1,0:T(8,128)(2,1)}, u32[]{:S(2)}, u32[]{:S(2)}) async-start(bf16[256,16,1024]{2,1,0:T(8,128)(2,1)} %bitcast.34), calls=%async_computation | async-start | bytes 16777216 | tf_op jit(solution)/shard_map/all_to_all | solution.py:34
  75.5 178.7 %reduce-scatter.2.cloned.1.call-start = ((), (), s32[]{:S(2)}) async-start(), calls=%async_computation.5 | async-start | bytes 4718592 | tf_op jit(solution)/shard_map/reduce_scatter | solution.py:46
  216.5 8.6 %copy-start.2 = (u32[256]{0:T(256)S(1)}, u32[256]{0:T(256)}, u32[]{:S(2)}) copy-start(u32[256]{0:T(256)} %constant.89) | copy-start | bytes 3076
  219.0 37.4 %all-to-all-start.1 = ((bf16[8,512,256]{2,0,1:T(8,128)(2,1)}), bf16[8,512,256]{2,0,1:T(8,128)(2,1)S(1)}, u32[]{:S(2)}, u32[]{:S(2)}) async-start(bf16[8,512,256]{2,0,1:T(8,128)(2,1)} %copy.14), calls=%async_computation.1 | async-start | bytes 4194304 | tf_op jit(solution)/shard_map/all_to_all | solution.py:44
  256.4 4.8 %copy-start = (bf16[8,512,256]{2,0,1:T(8,128)(2,1)}, bf16[8,512,256]{2,0,1:T(8,128)(2,1)S(1)}, u32[]{:S(2)}) copy-start(bf16[8,512,256]{2,0,1:T(8,128)(2,1)S(1)} %all-to-all-done.1) | copy-start | bytes 6291460
  256.4 16.1 %all-to-all-start.3 = ((bf16[256,8,128]{2,0,1:T(8,128)(2,1)}), bf16[256,8,128]{2,0,1:T(8,128)(2,1)S(1)}, u32[]{:S(2)}, u32[]{:S(2)}) async-start(bf16[256,8,128]{2,0,1:T(8,128)(2,1)} %copy_bitcast_fusion), calls=%async_computation.4 | async-start | bytes 1048576 | tf_op jit(solution)/shard_map/all_to_all | solution.py:50
Sparse Core Ops, SparseCore 0:
  10.3 57.6 all-gather.2
  201.0 53.1 reduce-scatter.1

commit v3 on v1

v3 whole, which is shorter than its diff:
```python
import functools

import jax
import jax.numpy as jnp
from jax import lax
from jax.experimental import pallas as pl
from jax.experimental.pallas import tpu as pltpu
from jax.sharding import Mesh, PartitionSpec as P

BS = 256
NZ = 8
PIECES = 2
DEPTH = 16
MESH = pl.DeviceIdType.MESH
F32, BF16 = jnp.float32, jnp.bfloat16
NT = (((1,), (1,)), ((), ()))


def kernel(
    dims, slots_row, slots_col, finals_row, points, centroids, dist_out, fresh_out,
    sendbuf, recvbuf, table, sums, partial, dsend, dret, rsend, rrecv, tsend, trecv, tall,
    csend, crecv, cnorm, denom, fsend, frecv, acc,
    p_send, p_recv, t_send, t_recv, d_send, d_recv, g_send, g_recv, r_send, r_recv,
    c_send, c_recv, f_send, f_recv, local_sem,
):
    nx, nc, ny = dims
    ng = nx * nc
    slab = ng * ny
    x, c, z, y = (lax.axis_index(a) for a in ("x", "core", "z", "y"))
    g = x * nc + c
    me = g * ny + y
    npoints, width = points.shape
    cols = width // PIECES
    chunk = NZ * DEPTH
    nrow = slab * DEPTH
    per = 128 // DEPTH

    def at(d):
        g2 = d // ny
        return (g2 // nc, g2 % nc, z, d % ny)

    def along(step):
        return (x, c, (z + step + NZ) % NZ, y)

    def remote(src, dst, ssem, rsem, dev):
        return pltpu.make_async_remote_copy(
            src_ref=src, dst_ref=dst, send_sem=ssem, recv_sem=rsem, device_id=dev, device_id_type=MESH
        )

    def point_copy(h, d, slot):
        return remote(sendbuf.at[h, d], recvbuf.at[h, slot], p_send.at[h, d], p_recv.at[h, slot], at(d))

    def target_copy(d, slot):
        return remote(tsend.at[d], trecv.at[slot], t_send.at[d], t_recv.at[slot], at(d))

    def dist_copy(d, slot):
        return remote(dsend.at[d], dret.at[slot], d_send.at[d], d_recv.at[slot], at(d))

    def count_copy(z2, slot):
        return remote(csend.at[z2], crecv.at[slot], c_send.at[z2], c_recv.at[slot], (x, c, z2, y))

    def fresh_copy(g2, slot):
        return remote(fsend.at[g2], frecv.at[slot], f_send.at[g2], f_recv.at[slot], (g2 // nc, g2 % nc, z, y))

    def others(n, own, fn):
        def body(i, _):
            @pl.when(i != own)
            def _():
                fn(i)

            return 0

        lax.fori_loop(0, n, body, 0)

    barrier = pltpu.get_barrier_semaphore()
    others(slab, me, lambda d: pl.semaphore_signal(barrier, inc=1, device_id=at(d), device_id_type=MESH))
    others(
        NZ, z, lambda z2: pl.semaphore_signal(barrier, inc=1, device_id=(x, c, z2, y), device_id_type=MESH)
    )
    own_copy = pltpu.make_async_copy(
        centroids.at[pl.ds(pl.multiple_of(g * BS, BS), BS)], table.at[z], local_sem
    )
    own_copy.start()

    slots = slots_row[...]
    dest = lax.shift_right_logical(slots, 4)
    rank = slots - dest * DEPTH
    value = (finals_row[...] + 1).astype(F32)
    which = lax.broadcasted_iota(jnp.int32, (slab * NZ, npoints), 0) == dest
    place = lax.broadcasted_iota(jnp.int32, (128, npoints), 0) == rank + (me % per) * DEPTH
    tiles = lax.dot_general(
        jnp.where(which, value, 0.0).astype(BF16), jnp.where(place, 1.0, 0.0).astype(BF16), NT,
        preferred_element_type=F32,
    )
    tsend[...] = tiles.reshape(slab, NZ, 128)
    trecv[me] = tsend[me]
    own_copy.wait()
    pl.semaphore_wait(barrier, slab - 1 + NZ - 1)
    others(slab, me, lambda d: target_copy(d, me).start())

    def ring_copy(way, step, back):
        step_z = 1 if way == 0 else -1
        owner = (z - step_z * (step - back) + 2 * NZ) % NZ if not back else (z - step_z * (step + 1) + 2 * NZ) % NZ
        rows = slice(None) if step < 3 else pl.ds(way * (BS // 2), BS // 2)
        ref = table.at[owner, rows] if step == 3 else table.at[owner]
        return remote(ref, ref, g_send.at[way, step], g_recv.at[way, step], along(step_z))

    def ring_step(step):
        for way in range(2):
            if step:
                ring_copy(way, step - 1, 1).wait_recv()
            if step < 4:
                ring_copy(way, step, 0).start()

    ring_step(0)

    def dispatch(h):
        def body(i, _):
            turn = (2 * (i % nx) + 1) % 5 if nx == 4 else i % nx
            g2 = ((x + turn) % nx) * nc + (c + i // nx) % nc
            hot = lax.broadcasted_iota(jnp.int32, (ny * chunk, npoints), 0) + g2 * (ny * chunk) == slots_row[...]
            moved = jnp.dot(
                jnp.where(hot, 1.0, 0.0).astype(BF16), points[:, h * cols : (h + 1) * cols],
                preferred_element_type=F32,
            ).astype(BF16)
            sendbuf[h, pl.ds(g2 * ny, ny)] = moved.reshape(ny, chunk, cols)
            for dy in range(ny):
                d = g2 * ny + (y + dy) % ny

                @pl.when(d != me)
                def _():
                    point_copy(h, d, me).start()

            return 0

        lax.fori_loop(0, ng, body, 0)
        recvbuf[h, me] = sendbuf[h, me]

    for h in range(PIECES):
        dispatch(h)
        ring_step(h + 1)
    for step in range(PIECES + 1, 5):
        ring_step(step)

    others(slab, me, lambda s: target_copy(s, s).wait_recv())
    for q in range(max(1, slab // per)):
        tile = trecv[q * per]
        for s in range(q * per + 1, min(slab, (q + 1) * per)):
            tile = tile + trecv[s]
        tall[:, q * 128 : (q + 1) * 128] = tile

    def norms(j, _):
        block = table[j].astype(F32)
        column = jnp.sum(block * block, axis=1, keepdims=True)
        cnorm[j] = jnp.broadcast_to(column, (BS, 128)).T[:8]
        return 0

    lax.fori_loop(0, NZ, norms, 0)

    def rows_of(h, j):
        return recvbuf[h, :, pl.ds(pl.multiple_of(j * DEPTH, DEPTH), DEPTH), :].reshape(nrow, cols)

    def add_up(h):
        def body(j, _):
            want = tall[pl.ds(j, 1), :][:, :nrow]
            centroid = lax.broadcasted_iota(jnp.int32, (BS, nrow), 0).astype(F32) + 1.0
            hot = jnp.where(want == centroid, 1.0, 0.0).astype(BF16)
            sums[j, :, h * cols : (h + 1) * cols] = jnp.dot(hot, rows_of(h, j), preferred_element_type=F32)
            if h == 0:
                csend[j] = lax.dot_general(jnp.ones((8, nrow), BF16), hot, NT, preferred_element_type=F32)
            return 0

        lax.fori_loop(0, NZ, body, 0)

    def measure(h):
        def body(j, _):
            rows = rows_of(h, j)
            wide = rows.astype(F32)
            cross = lax.dot_general(
                rows, table[j, :, h * cols : (h + 1) * cols], NT, preferred_element_type=F32
            )
            part = jnp.sum(wide * wide, axis=1, keepdims=True) - 2.0 * cross
            if h > 0:
                part = part + partial[j]
            if h < PIECES - 1:
                partial[j] = part
            else:
                whole = (part + cnorm[j, :1, :]) / width
                dsend[:, pl.ds(pl.multiple_of(j * DEPTH, DEPTH), DEPTH), :] = whole.astype(BF16).reshape(
                    slab, DEPTH, BS
                )
            return 0

        lax.fori_loop(0, NZ, body, 0)

    half = BS // 2

    def reduce_copy(h, way, step):
        rows = pl.ds(way * half, half)
        src = rsend.at[h, way, step, rows] if step == 0 else rsend.at[h, way, step]
        dst = rrecv.at[h, way, step, rows] if step == 0 else rrecv.at[h, way, step]
        return remote(src, dst, r_send.at[h, way, step], r_recv.at[h, way, step], along(1 if way == 0 else -1))

    def reduce_step(h, step):
        piece = slice(h * cols, (h + 1) * cols)
        for way in range(2):
            lo, hi = way * half, (way + 1) * half
            if step == 0:
                rsend[h, way, 0, lo:hi] = sums[(z + 4) % NZ, lo:hi, piece].astype(BF16)
            else:
                target = (z + 4 - step) % NZ if way == 0 else (z + 4 + step) % NZ
                reduce_copy(h, way, step - 1).wait_recv()
                if step == 1:
                    olo, ohi = (1 - way) * half, (2 - way) * half
                    rsend[h, way, 1, lo:hi] = (
                        sums[target, lo:hi, piece] + rrecv[h, way, 0, lo:hi].astype(F32)
                    ).astype(BF16)
                    rsend[h, way, 1, olo:ohi] = sums[target, olo:ohi, piece].astype(BF16)
                else:
                    rsend[h, way, step] = (
                        sums[target, :, piece] + rrecv[h, way, step - 1].astype(F32)
                    ).astype(BF16)
            reduce_copy(h, way, step).start()

    def finish(h):
        piece = slice(h * cols, (h + 1) * cols)
        for way in range(2):
            reduce_copy(h, way, 3).wait_recv()
        if h == 0:
            others(NZ, z, lambda z2: count_copy(z2, z2).wait_recv())
            total = csend[z]
            crecv[z] = total
            total = crecv[0]
            for z2 in range(1, NZ):
                total = total + crecv[z2]
            denom[...] = jnp.broadcast_to(total[:1], (128, BS)).T + 1.0
        own = (
            sums[z, :, piece] + rrecv[h, 0, 3].astype(F32) + rrecv[h, 1, 3].astype(F32)
            + table[z, :, piece].astype(F32)
        )
        share = width // ng
        for q in range(cols // share):
            g2 = h * (cols // share) + q
            fsend[g2] = (own[:, q * share : (q + 1) * share] / denom[:, :share]).astype(BF16)

            @pl.when(g2 != g)
            def _():
                fresh_copy(g2, g).start()

    for h in range(PIECES):
        others(slab, me, lambda s: point_copy(h, s, s).wait_recv())
        add_up(h)
        if h == 0:
            others(NZ, z, lambda z2: count_copy(z2, z).start())
        reduce_step(h, 0)
        measure(h)
        if h == PIECES - 1:
            others(slab, me, lambda d: dist_copy(d, me).start())
            dret[me] = dsend[me]
        for step in range(1, 4):
            reduce_step(h, step)
        finish(h)

    def bring(i, _):
        turn = (2 * (i % nx) + 1) % 5 if nx == 4 else i % nx
        g2 = ((x + turn) % nx) * nc + (c + i // nx) % nc
        for dy in range(ny):
            d = g2 * ny + dy

            @pl.when(d != me)
            def _():
                dist_copy(d, d).wait_recv()

        hot = lax.broadcasted_iota(jnp.int32, (npoints, ny * chunk), 1) + g2 * (ny * chunk) == slots_col[...]
        part = jnp.dot(
            jnp.where(hot, 1.0, 0.0).astype(BF16), dret[pl.ds(g2 * ny, ny)].reshape(ny * chunk, BS),
            preferred_element_type=F32,
        )

        @pl.when(i == 0)
        def _():
            acc[...] = part

        @pl.when(i > 0)
        def _():
            acc[...] += part

        return 0

    lax.fori_loop(0, ng, bring, 0)
    dist_out[...] = acc[...].astype(BF16)

    others(ng, g, lambda g2: fresh_copy(g2, g2).wait_recv())
    frecv[g] = fsend[g]
    for g2 in range(ng):
        fresh_out[g2 * BS : (g2 + 1) * BS, :] = frecv[g2].astype(F32)

    others(slab, me, lambda d: target_copy(d, me).wait_send())
    others(slab, me, lambda d: dist_copy(d, me).wait_send())
    others(NZ, z, lambda z2: count_copy(z2, z).wait_send())
    others(ng, g, lambda g2: fresh_copy(g2, g).wait_send())
    for way in range(2):
        for step in range(4):
            ring_copy(way, step, 0).wait_send()
    for h in range(PIECES):
        others(slab, me, lambda d: point_copy(h, d, me).wait_send())
        for way in range(2):
            for step in range(4):
                reduce_copy(h, way, step).wait_send()


def fused(slots, finals, points, centroids, dims):
    nx, nc, ny = dims
    ng, slab = nx * nc, nx * nc * ny
    npoints, width = points.shape
    cols, chunk, share = width // PIECES, NZ * DEPTH, width // (nx * nc)
    vmem, dma = pltpu.VMEM, pltpu.SemaphoreType.DMA
    tall_lanes = max(1, slab * DEPTH // 128) * 128
    return pl.pallas_call(
        functools.partial(kernel, dims),
        out_shape=(
            jax.ShapeDtypeStruct((npoints, BS), BF16),
            jax.ShapeDtypeStruct((ng * BS, share), F32),
        ),
        in_specs=[pl.BlockSpec(memory_space=vmem)] * 4 + [pl.BlockSpec(memory_space=pl.ANY)],
        out_specs=(pl.BlockSpec(memory_space=vmem),) * 2,
        scratch_shapes=[
            vmem((PIECES, slab, chunk, cols), BF16),
            vmem((PIECES, slab, chunk, cols), BF16),
            vmem((NZ, BS, width), BF16),
            vmem((NZ, BS, width), F32),
            vmem((NZ, slab * DEPTH, BS), F32),
            vmem((slab, chunk, BS), BF16),
            vmem((slab, chunk, BS), BF16),
            vmem((PIECES, 2, 4, BS, cols), BF16),
            vmem((PIECES, 2, 4, BS, cols), BF16),
            vmem((slab, NZ, 128), F32),
            vmem((slab, NZ, 128), F32),
            vmem((NZ, tall_lanes), F32),
            vmem((NZ, 8, BS), F32),
            vmem((NZ, 8, BS), F32),
            vmem((NZ, 8, BS), F32),
            vmem((BS, 128), F32),
            vmem((ng, BS, share), BF16),
            vmem((ng, BS, share), BF16),
            vmem((npoints, BS), F32),
            dma((PIECES, slab)), dma((PIECES, slab)), dma((slab,)), dma((slab,)), dma((slab,)), dma((slab,)),
            dma((2, 4)), dma((2, 4)), dma((PIECES, 2, 4)), dma((PIECES, 2, 4)),
            dma((NZ,)), dma((NZ,)), dma((ng,)), dma((ng,)), dma,
        ],
        compiler_params=pltpu.CompilerParams(
            collective_id=0, has_side_effects=True, vmem_limit_bytes=67043328
        ),
    )(slots[None, :], slots[:, None], finals[None, :], points, centroids)


def shards(points, blocks, finals, centroids):
    npoints, width = points.shape
    owned = centroids.shape[0] // BS
    dims = tuple(lax.axis_size(a) for a in ("x", "core", "y"))
    ny = dims[2]
    nblocks = owned * NZ * ny
    block_ids = blocks[:, 0]
    dest = ((block_ids % owned) * ny + (block_ids // owned) % ny) * NZ + block_ids // (owned * ny)
    labels = jnp.arange(nblocks, dtype=jnp.int32)
    member = dest[:, None] == labels[None, :]
    lower = (jnp.arange(npoints)[:, None] > jnp.arange(npoints)[None, :]).astype(BF16)
    before = jnp.dot(lower, member.astype(BF16), preferred_element_type=F32)
    ranks = jnp.sum(jnp.where(member, before, 0.0), axis=1).astype(jnp.int32)
    slots = dest * DEPTH + ranks
    return fused(slots, finals, points, centroids, dims)


def solution(mesh):
    ngrp, ndev = mesh.shape["grp"], mesh.shape["dev"]
    fine = Mesh(mesh.devices.reshape(ngrp // 2, 2, NZ, ndev // NZ), ("x", "core", "z", "y"))
    rows = ("x", "core", "z", "y")
    return jax.shard_map(
        shards,
        mesh=fine,
        in_specs=(P(rows, None), P(rows, None), P(rows), P(("z", "y"), None)),
        out_specs=(P(rows, None), P(("z", "y"), ("x", "core"))),
        check_vma=False,
    )
```

time: 355 us -> 187 us (0.53)
  the two profiles are of different devices: /device:TPU:6 before, /device:TPU:149 now
where the time goes in v3:
time: 187 us
  Pallas kernels  174 us (93%)
  local copies, waits for them, and re-layouts  5.23 us (3%)
  other arithmetic  4.53 us (2%)
  matrix products  2.41 us (1%)
    pallas_call x1, Pallas kernels, fused(): pl.pallas_call(functools.partial(kernel, dims), out_shape=(jax.ShapeDtype...  174 us
    unnamed x7, local copies, waits for them, and re-layouts  4.39 us

profile of v3, /device:TPU:149, one launch (start us, length us, event | category | flops | bytes accessed | tf_op | source)
XLA Modules:
  0.0 186.9 jit_solution(17859144304767176811)
XLA Ops:
  0.6 0.7 broadcast_compare_fusion
  1.3 0.5 copy.19
  1.8 1.1 copy.16
  2.9 2.0 %fusion.17 = (s32[2048]{0:T(1024)S(1)}, s32[2048,1]{1,0:T(8,128)S(1)}) fusion(pred[2048,1]{1,0:T(8,128)(4,1)S(1)} %copy.19, s32[2048,1]{1,0:T(8,128)S(1)} %copy.16), kind=kLoop, calls=%fused_computation.47 | loop fusion | flops 88064 | bytes 26624 | tf_op jit(solution)/shard_map/add | solution.py:364
  4.9 0.0 copy-start.1
  4.9 2.4 %fusion.2 = f32[2048]{0:T(1024)S(1)} fusion(s32[2048]{0:T(1024)S(1)} %get-tuple-element.2), kind=kOutput, calls=%fused_computation.15 | convolution fusion | flops 2153773056 | bytes 16384 | tf_op jit(solution)/shard_map/dot_general | solution.py:368
  7.3 0.0 copy-done.1
  7.3 0.7 multiply_add_fusion.1.slots_row
  8.1 0.4 copy.24
  8.4 1.1 multiply_add_fusion.slots_col
  9.5 174.0 %shard_map.59 = (bf16[2048,256]{1,0:T(8,128)(2,1)}, f32[2048,128]{1,0:T(8,128)}) custom-call(s32[1,2048]{1,0:T(1,128)} %multiply_add_fusion.1.slots_row, s32[2048,1]{1,0:T(8,128)} %multiply_add_fusion.slots_col, s32[1,2048]{1,0:T(1,128)} %bitcast.21, bf16[2048,1024]{1,0:T(8,128)(2,1)} %points.1, bf16[2048,1024]{1,0:T(8,128)(2,1)} %centroids.1), custom_call_target="tpu_custom_call" | custom-call | tf_op jit(solution)/shard_map/pallas_call | solution.py:319
  183.5 0.0 copy-start
  183.6 2.4 %copy.27 = bf16[2048,256]{1,0:T(8,128)(2,1)} copy(bf16[2048,256]{1,0:T(8,128)(2,1)} %get-tuple-element.6) | data formatting | bytes 2097152
  185.9 0.0 copy-done
  185.9 1.0 copy.28
  (1 shorter events, 0.0 us)
Async XLA Ops:
  4.9 2.4 %copy-start.1 = (s32[2048,1]{0,1:T(1,128)S(1)}, s32[2048,1]{0,1:T(1,128)}, u32[]{:S(2)}) copy-start(s32[2048,1]{0,1:T(1,128)} %param.5) | copy-start | bytes 24580
  183.5 2.4 %copy-start = (f32[2048,128]{1,0:T(8,128)S(1)}, f32[2048,128]{1,0:T(8,128)}, u32[]{:S(2)}) copy-start(f32[2048,128]{1,0:T(8,128)} %get-tuple-element.7) | copy-start | bytes 3145732

commit v4 on v3

v4 whole, which is shorter than its diff:
```python
import functools

import jax
import jax.numpy as jnp
from jax import lax
from jax.experimental import pallas as pl
from jax.experimental.pallas import tpu as pltpu
from jax.sharding import Mesh, PartitionSpec as P

BS = 256
NZ = 8
SPLIT = (4, 2, 2)
DEPTH = 16
MESH = pl.DeviceIdType.MESH
F32, BF16 = jnp.float32, jnp.bfloat16
NT = (((1,), (1,)), ((), ()))


def kernel(
    dims, blocks_row, finals_row, points, centroids, dist_out, fresh_out,
    sendbuf, recvbuf, rsend, rrecv, table, sums, partial, dsend, dret, tsend, trecv, tall,
    csend, crecv, cnorm, denom, fsend, acc, slots_row, slots_col,
    p_send, p_recv, t_send, t_recv, d_send, d_recv, g_send, g_recv, r_send, r_recv,
    c_send, c_recv, f_send, f_recv, local_sem,
):
    nx, nc, ny = dims
    ng = nx * nc
    slab = ng * ny
    x, c, z, y = (lax.axis_index(a) for a in ("x", "core", "z", "y"))
    g = x * nc + c
    me = g * ny + y
    npoints, width = points.shape
    pieces = [slice(a, b) for a, b in bounds(width)]
    frecv = fresh_out
    chunk = NZ * DEPTH
    nrow = slab * DEPTH
    per = 128 // DEPTH

    def at(d):
        g2 = d // ny
        return (g2 // nc, g2 % nc, z, d % ny)

    def along(step):
        return (x, c, (z + step + NZ) % NZ, y)

    def remote(src, dst, ssem, rsem, dev):
        return pltpu.make_async_remote_copy(
            src_ref=src, dst_ref=dst, send_sem=ssem, recv_sem=rsem, device_id=dev, device_id_type=MESH
        )

    def point_copy(h, d, slot):
        return remote(sendbuf[h].at[d], recvbuf[h].at[slot], p_send.at[h, d], p_recv.at[h, slot], at(d))

    def target_copy(d, slot):
        return remote(tsend.at[d], trecv.at[slot], t_send.at[d], t_recv.at[slot], at(d))

    def dist_copy(d, slot):
        return remote(dsend.at[d], dret.at[slot], d_send.at[d], d_recv.at[slot], at(d))

    def count_copy(z2, slot):
        return remote(csend.at[z2], crecv.at[slot], c_send.at[z2], c_recv.at[slot], (x, c, z2, y))

    def fresh_copy(g2, slot):
        return remote(fsend.at[g2], frecv.at[slot], f_send.at[g2], f_recv.at[slot], (g2 // nc, g2 % nc, z, y))

    def others(n, own, fn):
        def body(i, _):
            @pl.when(i != own)
            def _():
                fn(i)

            return 0

        lax.fori_loop(0, n, body, 0)

    def offset(i):
        turn = (2 * (i % nx) + 1) % 5 if nx == 4 else i % nx
        return turn, i // nx

    barrier = pltpu.get_barrier_semaphore()
    others(slab, me, lambda d: pl.semaphore_signal(barrier, inc=1, device_id=at(d), device_id_type=MESH))
    others(
        NZ, z, lambda z2: pl.semaphore_signal(barrier, inc=1, device_id=(x, c, z2, y), device_id_type=MESH)
    )
    own_copy = pltpu.make_async_copy(
        centroids.at[pl.ds(pl.multiple_of(g * BS, BS), BS)], table.at[z], local_sem
    )
    own_copy.start()

    ids = blocks_row[...]
    dest = ((ids & (ng - 1)) * ny + (lax.shift_right_logical(ids, ng.bit_length() - 1) & (ny - 1))) * NZ
    dest = dest + lax.shift_right_logical(ids, (ng * ny).bit_length() - 1)
    strip = min(256, npoints)
    earlier = lax.broadcasted_iota(jnp.int32, (strip, strip), 0) < lax.broadcasted_iota(jnp.int32, (strip, strip), 1)
    earlier = jnp.where(earlier, 1.0, 0.0).astype(BF16)
    seen = jnp.zeros((slab * NZ, 1), F32)
    ranks = []
    for q in range(npoints // strip):
        part = dest[:, q * strip : (q + 1) * strip]
        member = jnp.where(lax.broadcasted_iota(jnp.int32, (slab * NZ, strip), 0) == part, 1.0, 0.0)
        before = jnp.dot(member.astype(BF16), earlier, preferred_element_type=F32) + seen
        ranks.append(jnp.sum(member * before, axis=0, keepdims=True))
        seen = seen + jnp.sum(member, axis=1, keepdims=True)
    rank = jnp.concatenate(ranks, axis=1).astype(jnp.int32)
    slots = dest * DEPTH + rank
    slots_row[...] = slots
    slots_col[...] = jnp.broadcast_to(slots.astype(F32), (128, npoints)).T.astype(jnp.int32)

    value = (finals_row[...] + 1).astype(F32)
    which = lax.broadcasted_iota(jnp.int32, (slab * NZ, npoints), 0) == dest
    place = lax.broadcasted_iota(jnp.int32, (128, npoints), 0) == rank + (me % per) * DEPTH
    tiles = lax.dot_general(
        jnp.where(which, value, 0.0).astype(BF16), jnp.where(place, 1.0, 0.0).astype(BF16), NT,
        preferred_element_type=F32,
    )
    tsend[...] = tiles.reshape(slab, NZ, 128)
    trecv[me] = tsend[me]
    own_copy.wait()
    pl.semaphore_wait(barrier, slab - 1 + NZ - 1)
    others(slab, me, lambda d: target_copy(d, me).start())

    def ring_copy(way, step, back):
        step_z = 1 if way == 0 else -1
        owner = (z - step_z * (step - back) + 2 * NZ) % NZ if not back else (z - step_z * (step + 1) + 2 * NZ) % NZ
        rows = slice(None) if step < 3 else pl.ds(way * (BS // 2), BS // 2)
        ref = table.at[owner, rows] if step == 3 else table.at[owner]
        return remote(ref, ref, g_send.at[way, step], g_recv.at[way, step], along(step_z))

    def ring_step(step):
        for way in range(2):
            if step:
                ring_copy(way, step - 1, 1).wait_recv()
            if step < 4:
                ring_copy(way, step, 0).start()

    ring_step(0)

    def dispatch(h):
        def body(i, _):
            dx, dc = offset(i)
            g2 = ((x + dx) % nx) * nc + (c + dc) % nc
            hot = lax.broadcasted_iota(jnp.int32, (ny * chunk, npoints), 0) + g2 * (ny * chunk) == slots_row[...]
            moved = jnp.dot(
                jnp.where(hot, 1.0, 0.0).astype(BF16), points[:, pieces[h]],
                preferred_element_type=F32,
            ).astype(BF16)
            sendbuf[h][pl.ds(g2 * ny, ny)] = moved.reshape(ny, chunk, moved.shape[1])
            for dy in range(ny):
                d = g2 * ny + (y + dy) % ny

                @pl.when(d != me)
                def _():
                    point_copy(h, d, me).start()

            return 0

        lax.fori_loop(0, ng, body, 0)
        recvbuf[h][me] = sendbuf[h][me]

    for h in range(len(pieces)):
        dispatch(h)
        ring_step(h + 1)
    for step in range(len(pieces) + 1, 5):
        ring_step(step)

    others(slab, me, lambda s: target_copy(s, s).wait_recv())
    for q in range(max(1, slab // per)):
        tile = trecv[q * per]
        for s in range(q * per + 1, min(slab, (q + 1) * per)):
            tile = tile + trecv[s]
        tall[:, q * 128 : (q + 1) * 128] = tile

    def norms(j, _):
        block = table[j].astype(F32)
        column = jnp.sum(block * block, axis=1, keepdims=True)
        cnorm[j] = jnp.broadcast_to(column, (BS, 128)).T[:8]
        return 0

    lax.fori_loop(0, NZ, norms, 0)

    def rows_of(h, j):
        return recvbuf[h][:, pl.ds(pl.multiple_of(j * DEPTH, DEPTH), DEPTH), :].reshape(nrow, -1)

    def add_up(h):
        def body(j, _):
            want = tall[pl.ds(j, 1), :][:, :nrow]
            centroid = lax.broadcasted_iota(jnp.int32, (BS, nrow), 0).astype(F32) + 1.0
            hot = jnp.where(want == centroid, 1.0, 0.0).astype(BF16)
            sums[j, :, pieces[h]] = jnp.dot(hot, rows_of(h, j), preferred_element_type=F32)
            if h == 0:
                csend[j] = lax.dot_general(jnp.ones((8, nrow), BF16), hot, NT, preferred_element_type=F32)
            return 0

        lax.fori_loop(0, NZ, body, 0)

    def measure(h):
        def body(j, _):
            rows = rows_of(h, j)
            wide = rows.astype(F32)
            cross = lax.dot_general(
                rows, table[j, :, pieces[h]], NT, preferred_element_type=F32
            )
            part = jnp.sum(wide * wide, axis=1, keepdims=True) - 2.0 * cross
            if h > 0:
                part = part + partial[j]
            if h < len(pieces) - 1:
                partial[j] = part
            else:
                whole = (part + cnorm[j, :1, :]) / width
                dsend[:, pl.ds(pl.multiple_of(j * DEPTH, DEPTH), DEPTH), :] = whole.astype(BF16).reshape(
                    slab, DEPTH, BS
                )
            return 0

        lax.fori_loop(0, NZ, body, 0)

    half = BS // 2

    def reduce_copy(h, way, step):
        rows = pl.ds(way * half, half)
        src = rsend[h].at[way, step, rows] if step == 0 else rsend[h].at[way, step]
        dst = rrecv[h].at[way, step, rows] if step == 0 else rrecv[h].at[way, step]
        return remote(src, dst, r_send.at[h, way, step], r_recv.at[h, way, step], along(1 if way == 0 else -1))

    def reduce_step(h, step):
        piece = pieces[h]
        for way in range(2):
            lo, hi = way * half, (way + 1) * half
            if step == 0:
                rsend[h][way, 0, lo:hi] = sums[(z + 4) % NZ, lo:hi, piece].astype(BF16)
            else:
                target = (z + 4 - step) % NZ if way == 0 else (z + 4 + step) % NZ
                reduce_copy(h, way, step - 1).wait_recv()
                if step == 1:
                    olo, ohi = (1 - way) * half, (2 - way) * half
                    rsend[h][way, 1, lo:hi] = (
                        sums[target, lo:hi, piece] + rrecv[h][way, 0, lo:hi].astype(F32)
                    ).astype(BF16)
                    rsend[h][way, 1, olo:ohi] = sums[target, olo:ohi, piece].astype(BF16)
                else:
                    rsend[h][way, step] = (
                        sums[target, :, piece] + rrecv[h][way, step - 1].astype(F32)
                    ).astype(BF16)
            reduce_copy(h, way, step).start()

    def finish(h):
        piece = pieces[h]
        for way in range(2):
            reduce_copy(h, way, 3).wait_recv()
        if h == 0:
            others(NZ, z, lambda z2: count_copy(z2, z2).wait_recv())
            total = csend[z]
            crecv[z] = total
            total = crecv[0]
            for z2 in range(1, NZ):
                total = total + crecv[z2]
            denom[...] = jnp.broadcast_to(total[:1], (128, BS)).T + 1.0
        own = (
            sums[z, :, piece] + rrecv[h][0, 3].astype(F32) + rrecv[h][1, 3].astype(F32)
            + table[z, :, piece].astype(F32)
        )
        share = width // ng
        for q in range(own.shape[1] // share):
            g2 = piece.start // share + q
            fsend[g2] = (own[:, q * share : (q + 1) * share] / denom[:, :share]).astype(BF16)

            @pl.when(g2 != g)
            def _():
                fresh_copy(g2, g).start()

    def give_back(i, _):
        dx, dc = offset(i)
        g2 = ((x + dx) % nx) * nc + (c + dc) % nc
        for dy in range(ny):
            d = g2 * ny + (y + dy) % ny

            @pl.when(d != me)
            def _():
                dist_copy(d, me).start()

        return 0

    for h in range(len(pieces)):
        others(slab, me, lambda s: point_copy(h, s, s).wait_recv())
        add_up(h)
        if h == 0:
            others(NZ, z, lambda z2: count_copy(z2, z).start())
        reduce_step(h, 0)
        measure(h)
        if h == len(pieces) - 1:
            lax.fori_loop(0, ng, give_back, 0)
            dret[me] = dsend[me]
        for step in range(1, 4):
            reduce_step(h, step)
        finish(h)

    def bring(i, _):
        dx, dc = offset(i)
        g2 = ((x + nx - dx) % nx) * nc + (c + dc) % nc
        for dy in range(ny):
            d = g2 * ny + dy

            @pl.when(d != me)
            def _():
                dist_copy(d, d).wait_recv()

        hot = lax.broadcasted_iota(jnp.int32, (npoints, ny * chunk), 1) + g2 * (ny * chunk) == slots_col[:, :1]
        part = jnp.dot(
            jnp.where(hot, 1.0, 0.0).astype(BF16), dret[pl.ds(g2 * ny, ny)].reshape(ny * chunk, BS),
            preferred_element_type=F32,
        )

        @pl.when(i == 0)
        def _():
            acc[...] = part

        @pl.when(i > 0)
        def _():
            acc[...] += part

        return 0

    lax.fori_loop(0, ng, bring, 0)
    dist_out[...] = acc[...].astype(BF16)

    others(ng, g, lambda g2: fresh_copy(g2, g2).wait_recv())
    frecv[g] = fsend[g]

    others(slab, me, lambda d: target_copy(d, me).wait_send())
    others(slab, me, lambda d: dist_copy(d, me).wait_send())
    others(NZ, z, lambda z2: count_copy(z2, z).wait_send())
    others(ng, g, lambda g2: fresh_copy(g2, g).wait_send())
    for way in range(2):
        for step in range(4):
            ring_copy(way, step, 0).wait_send()
    for h in range(len(pieces)):
        others(slab, me, lambda d: point_copy(h, d, me).wait_send())
        for way in range(2):
            for step in range(4):
                reduce_copy(h, way, step).wait_send()


def bounds(width):
    edges = [0]
    for part in SPLIT:
        edges.append(edges[-1] + part * width // sum(SPLIT))
    return list(zip(edges[:-1], edges[1:]))


def fused(blocks, finals, points, centroids, dims):
    nx, nc, ny = dims
    ng, slab = nx * nc, nx * nc * ny
    npoints, width = points.shape
    chunk, share = NZ * DEPTH, width // (nx * nc)
    sizes = [b - a for a, b in bounds(width)]
    n = len(sizes)
    vmem, dma = pltpu.VMEM, pltpu.SemaphoreType.DMA
    tall_lanes = max(1, slab * DEPTH // 128) * 128
    return pl.pallas_call(
        functools.partial(kernel, dims),
        out_shape=(
            jax.ShapeDtypeStruct((npoints, BS), BF16),
            jax.ShapeDtypeStruct((ng, BS, share), BF16),
        ),
        in_specs=[pl.BlockSpec(memory_space=vmem)] * 3 + [pl.BlockSpec(memory_space=pl.ANY)],
        out_specs=(pl.BlockSpec(memory_space=vmem),) * 2,
        scratch_shapes=[
            tuple(vmem((slab, chunk, size), BF16) for size in sizes),
            tuple(vmem((slab, chunk, size), BF16) for size in sizes),
            tuple(vmem((2, 4, BS, size), BF16) for size in sizes),
            tuple(vmem((2, 4, BS, size), BF16) for size in sizes),
            vmem((NZ, BS, width), BF16),
            vmem((NZ, BS, width), F32),
            vmem((NZ, slab * DEPTH, BS), F32),
            vmem((slab, chunk, BS), BF16),
            vmem((slab, chunk, BS), BF16),
            vmem((slab, NZ, 128), F32),
            vmem((slab, NZ, 128), F32),
            vmem((NZ, tall_lanes), F32),
            vmem((NZ, 8, BS), F32),
            vmem((NZ, 8, BS), F32),
            vmem((NZ, 8, BS), F32),
            vmem((BS, 128), F32),
            vmem((ng, BS, share), BF16),
            vmem((npoints, BS), F32),
            vmem((1, npoints), jnp.int32),
            vmem((npoints, 128), jnp.int32),
            dma((n, slab)), dma((n, slab)), dma((slab,)), dma((slab,)), dma((slab,)), dma((slab,)),
            dma((2, 4)), dma((2, 4)), dma((n, 2, 4)), dma((n, 2, 4)),
            dma((NZ,)), dma((NZ,)), dma((ng,)), dma((ng,)), dma,
        ],
        compiler_params=pltpu.CompilerParams(
            collective_id=0, has_side_effects=True, vmem_limit_bytes=67043328
        ),
    )(blocks.reshape(1, npoints), finals[None, :], points, centroids)


def shards(points, blocks, finals, centroids):
    dims = tuple(lax.axis_size(a) for a in ("x", "core", "y"))
    distances, refreshed = fused(blocks, finals, points, centroids, dims)
    return distances, refreshed.reshape(-1, refreshed.shape[2]).astype(F32)


def solution(mesh):
    ngrp, ndev = mesh.shape["grp"], mesh.shape["dev"]
    fine = Mesh(mesh.devices.reshape(ngrp // 2, 2, NZ, ndev // NZ), ("x", "core", "z", "y"))
    rows = ("x", "core", "z", "y")
    return jax.shard_map(
        shards,
        mesh=fine,
        in_specs=(P(rows, None), P(rows, None), P(rows), P(("z", "y"), None)),
        out_specs=(P(rows, None), P(("z", "y"), ("x", "core"))),
        check_vma=False,
    )
```

time: 187 us -> 167 us (0.89)
  the two profiles are of different devices: /device:TPU:149 before, /device:TPU:6 now
where the time goes in v4:
time: 167 us; the launch traced here: 164 us
  Pallas kernels  159 us (95%)
  local copies, waits for them, and re-layouts  2.26 us (1%)
  other arithmetic  2.08 us (1%)
    pallas_call x1, Pallas kernels, fused(): pl.pallas_call(functools.partial(kernel, dims), out_shape=(jax.ShapeDtype...  159 us

profile of v4, /device:TPU:6, one launch (start us, length us, event | category | flops | bytes accessed | tf_op | source)
XLA Modules:
  0.0 164.0 jit_solution(2188335974973357601)
XLA Ops:
  0.6 159.0 %shard_map.59 = (bf16[2048,256]{1,0:T(8,128)(2,1)}, bf16[8,256,128]{2,1,0:T(8,128)(2,1)}) custom-call(s32[1,2048]{1,0:T(1,128)} %bitcast.5, s32[1,2048]{1,0:T(1,128)} %bitcast.6, bf16[2048,1024]{1,0:T(8,128)(2,1)} %points.1, bf16[2048,1024]{1,0:T(8,128)(2,1)} %centroids.1), custom_call_target="tpu_custom_call" | custom-call | tf_op jit(solution)/shard_map/pallas_call | solution.py:359
  159.7 2.1 %bitcast_convert_fusion = f32[2048,128]{1,0:T(8,128)} fusion(bf16[8,256,128]{2,1,0:T(8,128)(2,1)} %get-tuple-element.5), kind=kLoop, calls=%fused_computation | loop fusion | flops 262144 | bytes 1572864 | tf_op jit(solution)/shard_map/convert_element_type | solution.py:401
  161.7 2.3 %copy.7 = bf16[2048,256]{1,0:T(8,128)(2,1)} copy(bf16[2048,256]{1,0:T(8,128)(2,1)} %get-tuple-element.8) | data formatting | bytes 2097152

commit v5 on v4

--- a/solution.py
+++ b/solution.py
@@ -10,6 +10,7 @@
 BS = 256
 NZ = 8
 SPLIT = (4, 2, 2)
+ROOM = 112
 DEPTH = 16
 MESH = pl.DeviceIdType.MESH
 F32, BF16 = jnp.float32, jnp.bfloat16
@@ -17,11 +18,11 @@
 
 
 def kernel(
-    dims, blocks_row, finals_row, points, centroids, dist_out, fresh_out,
-    sendbuf, recvbuf, rsend, rrecv, table, sums, partial, dsend, dret, tsend, trecv, tall,
+    dims, room, blocks_row, finals_row, points_in, centroids, dist_out, fresh_out, flag_out,
+    points, sendbuf, recvbuf, opened, rsend, rrecv, table, sums, partial, dsend, dret, tsend, trecv, tall,
     csend, crecv, cnorm, denom, fsend, acc, slots_row, slots_col,
     p_send, p_recv, t_send, t_recv, d_send, d_recv, g_send, g_recv, r_send, r_recv,
-    c_send, c_recv, f_send, f_recv, local_sem,
+    c_send, c_recv, f_send, f_recv, local_sem, points_sem,
 ):
     nx, nc, ny = dims
     ng = nx * nc
@@ -86,6 +87,8 @@
         centroids.at[pl.ds(pl.multiple_of(g * BS, BS), BS)], table.at[z], local_sem
     )
     own_copy.start()
+    points_copy = pltpu.make_async_copy(points_in, points, points_sem)
+    points_copy.start()
 
     ids = blocks_row[...]
     dest = ((ids & (ng - 1)) * ny + (lax.shift_right_logical(ids, ng.bit_length() - 1) & (ny - 1))) * NZ
@@ -93,18 +96,36 @@
     strip = min(256, npoints)
     earlier = lax.broadcasted_iota(jnp.int32, (strip, strip), 0) < lax.broadcasted_iota(jnp.int32, (strip, strip), 1)
     earlier = jnp.where(earlier, 1.0, 0.0).astype(BF16)
+    strips = [dest[:, q * strip : (q + 1) * strip] for q in range(npoints // strip)]
+    members = [
+        jnp.where(lax.broadcasted_iota(jnp.int32, (slab * NZ, strip), 0) == part, 1.0, 0.0) for part in strips
+    ]
+    held = [jnp.sum(member, axis=1, keepdims=True) for member in members]
+    load = functools.reduce(lambda a, b: a + b, held)
+    above = lax.broadcasted_iota(jnp.int32, (slab * NZ, slab * NZ), 0)
+    left = lax.broadcasted_iota(jnp.int32, (slab * NZ, slab * NZ), 1)
+    prior = jnp.where((left < above) & (left // NZ == above // NZ), 1.0, 0.0).astype(BF16)
+    first = jnp.dot(
+        prior, jnp.broadcast_to(load, (slab * NZ, 128)).astype(BF16), preferred_element_type=F32
+    )[:, :1]
     seen = jnp.zeros((slab * NZ, 1), F32)
-    ranks = []
-    for q in range(npoints // strip):
-        part = dest[:, q * strip : (q + 1) * strip]
-        member = jnp.where(lax.broadcasted_iota(jnp.int32, (slab * NZ, strip), 0) == part, 1.0, 0.0)
+    ranks, firsts = [], []
+    for member, more in zip(members, held):
         before = jnp.dot(member.astype(BF16), earlier, preferred_element_type=F32) + seen
         ranks.append(jnp.sum(member * before, axis=0, keepdims=True))
-        seen = seen + jnp.sum(member, axis=1, keepdims=True)
+        firsts.append(jnp.sum(member * first, axis=0, keepdims=True))
+        seen = seen + more
     rank = jnp.concatenate(ranks, axis=1).astype(jnp.int32)
     slots = dest * DEPTH + rank
-    slots_row[...] = slots
     slots_col[...] = jnp.broadcast_to(slots.astype(F32), (128, npoints)).T.astype(jnp.int32)
+    compact = room < chunk
+    holder = lax.shift_right_logical(dest, NZ.bit_length() - 1)
+    if compact:
+        spot = rank + jnp.concatenate(firsts, axis=1).astype(jnp.int32)
+        over = jnp.max(jnp.where(spot >= room, 1.0, 0.0), axis=1, keepdims=True)
+        slots_row[...] = jnp.where(spot < room, holder * room + spot, -1)
+    else:
+        slots_row[...] = slots
 
     value = (finals_row[...] + 1).astype(F32)
     which = lax.broadcasted_iota(jnp.int32, (slab * NZ, npoints), 0) == dest
@@ -113,7 +134,17 @@
         jnp.where(which, value, 0.0).astype(BF16), jnp.where(place, 1.0, 0.0).astype(BF16), NT,
         preferred_element_type=F32,
     )
-    tsend[...] = tiles.reshape(slab, NZ, 128)
+    tsend[:, :NZ, :] = tiles.reshape(slab, NZ, 128)
+    if compact:
+        origin = (slots - holder * chunk + 1).astype(F32)
+        to = lax.broadcasted_iota(jnp.int32, (slab, npoints), 0) == holder
+        row = lax.broadcasted_iota(jnp.int32, (128, npoints), 0) == spot
+        origins = lax.dot_general(
+            jnp.where(to, origin, 0.0).astype(BF16), jnp.where(row, 1.0, 0.0).astype(BF16), NT,
+            preferred_element_type=F32,
+        )
+        line = lax.broadcasted_iota(jnp.int32, (slab, NZ, 128), 1)
+        tsend[:, NZ:, :] = jnp.where(line == 0, origins[:, None, :], over[None])
     trecv[me] = tsend[me]
     own_copy.wait()
     pl.semaphore_wait(barrier, slab - 1 + NZ - 1)
@@ -134,17 +165,18 @@
                 ring_copy(way, step, 0).start()
 
     ring_step(0)
+    points_copy.wait()
 
     def dispatch(h):
         def body(i, _):
             dx, dc = offset(i)
             g2 = ((x + dx) % nx) * nc + (c + dc) % nc
-            hot = lax.broadcasted_iota(jnp.int32, (ny * chunk, npoints), 0) + g2 * (ny * chunk) == slots_row[...]
+            hot = lax.broadcasted_iota(jnp.int32, (ny * room, npoints), 0) + g2 * (ny * room) == slots_row[...]
             moved = jnp.dot(
                 jnp.where(hot, 1.0, 0.0).astype(BF16), points[:, pieces[h]],
                 preferred_element_type=F32,
             ).astype(BF16)
-            sendbuf[h][pl.ds(g2 * ny, ny)] = moved.reshape(ny, chunk, moved.shape[1])
+            sendbuf[h][pl.ds(g2 * ny, ny)] = moved.reshape(ny, room, moved.shape[1])
             for dy in range(ny):
                 d = g2 * ny + (y + dy) % ny
 
@@ -178,17 +210,39 @@
 
     lax.fori_loop(0, NZ, norms, 0)
 
+    def expand(h):
+        size = pieces[h].stop - pieces[h].start
+
+        def body(i, _):
+            for k in range(4):
+                s = i * 4 + k
+                slot = lax.broadcasted_iota(jnp.int32, (chunk, room), 0).astype(F32) + 1.0
+                hot = jnp.where(trecv[s, NZ : NZ + 1, :room] == slot, 1.0, 0.0).astype(BF16)
+                opened[s, :, :size] = jnp.dot(hot, recvbuf[h][s], preferred_element_type=F32).astype(BF16)
+            return 0
+
+        if compact:
+            lax.fori_loop(0, slab // 4, body, 0)
+
     def rows_of(h, j):
+        size = pieces[h].stop - pieces[h].start
+        if compact:
+            return opened[:, pl.ds(pl.multiple_of(j * DEPTH, DEPTH), DEPTH), :size].reshape(nrow, size)
         return recvbuf[h][:, pl.ds(pl.multiple_of(j * DEPTH, DEPTH), DEPTH), :].reshape(nrow, -1)
 
     def add_up(h):
         def body(j, _):
-            want = tall[pl.ds(j, 1), :][:, :nrow]
+            want = tall[pl.ds(j, 1), :nrow]
             centroid = lax.broadcasted_iota(jnp.int32, (BS, nrow), 0).astype(F32) + 1.0
             hot = jnp.where(want == centroid, 1.0, 0.0).astype(BF16)
             sums[j, :, pieces[h]] = jnp.dot(hot, rows_of(h, j), preferred_element_type=F32)
             if h == 0:
-                csend[j] = lax.dot_general(jnp.ones((8, nrow), BF16), hot, NT, preferred_element_type=F32)
+                number = lax.dot_general(jnp.ones((8, nrow), BF16), hot, NT, preferred_element_type=F32)
+                if compact:
+                    line = lax.broadcasted_iota(jnp.int32, (8, BS), 0)
+                    short = jnp.sum(tall[NZ + 1 : NZ + 2, :], axis=1, keepdims=True)
+                    number = jnp.where(line == 0, number, short)
+                csend[j] = number
             return 0
 
         lax.fori_loop(0, NZ, body, 0)
@@ -254,6 +308,7 @@
             total = crecv[0]
             for z2 in range(1, NZ):
                 total = total + crecv[z2]
+            flag_out[...] = jnp.broadcast_to(total[1:2, :128], (8, 128))
             denom[...] = jnp.broadcast_to(total[:1], (128, BS)).T + 1.0
         own = (
             sums[z, :, piece] + rrecv[h][0, 3].astype(F32) + rrecv[h][1, 3].astype(F32)
@@ -280,19 +335,34 @@
 
         return 0
 
-    for h in range(len(pieces)):
+    def arrived(h):
         others(slab, me, lambda s: point_copy(h, s, s).wait_recv())
+
+    last = len(pieces) - 1
+    for h in range(last):
+        arrived(h)
+        expand(h)
         add_up(h)
         if h == 0:
             others(NZ, z, lambda z2: count_copy(z2, z).start())
         reduce_step(h, 0)
         measure(h)
-        if h == len(pieces) - 1:
-            lax.fori_loop(0, ng, give_back, 0)
-            dret[me] = dsend[me]
-        for step in range(1, 4):
+        for step in range(1, 4 if h < last - 1 else 3):
             reduce_step(h, step)
-        finish(h)
+        if h < last - 1:
+            finish(h)
+    arrived(last)
+    expand(last)
+    measure(last)
+    lax.fori_loop(0, ng, give_back, 0)
+    dret[me] = dsend[me]
+    add_up(last)
+    reduce_step(last, 0)
+    reduce_step(last - 1, 3)
+    finish(last - 1)
+    for step in range(1, 4):
+        reduce_step(last, step)
+    finish(last)
 
     def bring(i, _):
         dx, dc = offset(i)
@@ -347,7 +417,7 @@
     return list(zip(edges[:-1], edges[1:]))
 
 
-def fused(blocks, finals, points, centroids, dims):
+def fused(blocks, finals, points, centroids, dims, room, name):
     nx, nc, ny = dims
     ng, slab = nx * nc, nx * nc * ny
     npoints, width = points.shape
@@ -355,18 +425,22 @@
     sizes = [b - a for a, b in bounds(width)]
     n = len(sizes)
     vmem, dma = pltpu.VMEM, pltpu.SemaphoreType.DMA
+    lines = 2 * NZ if room < chunk else NZ
     tall_lanes = max(1, slab * DEPTH // 128) * 128
     return pl.pallas_call(
-        functools.partial(kernel, dims),
+        functools.partial(kernel, dims, room),
         out_shape=(
             jax.ShapeDtypeStruct((npoints, BS), BF16),
             jax.ShapeDtypeStruct((ng, BS, share), BF16),
+            jax.ShapeDtypeStruct((8, 128), F32),
         ),
-        in_specs=[pl.BlockSpec(memory_space=vmem)] * 3 + [pl.BlockSpec(memory_space=pl.ANY)],
-        out_specs=(pl.BlockSpec(memory_space=vmem),) * 2,
+        in_specs=[pl.BlockSpec(memory_space=vmem)] * 2 + [pl.BlockSpec(memory_space=pl.ANY)] * 2,
+        out_specs=(pl.BlockSpec(memory_space=vmem),) * 3,
         scratch_shapes=[
-            tuple(vmem((slab, chunk, size), BF16) for size in sizes),
-            tuple(vmem((slab, chunk, size), BF16) for size in sizes),
+            vmem((npoints, width), BF16),
+            tuple(vmem((slab, room, size), BF16) for size in sizes),
+            tuple(vmem((slab, room, size), BF16) for size in sizes),
+            vmem((slab, chunk, max(sizes)) if room < chunk else (8, 128), BF16),
             tuple(vmem((2, 4, BS, size), BF16) for size in sizes),
             tuple(vmem((2, 4, BS, size), BF16) for size in sizes),
             vmem((NZ, BS, width), BF16),
@@ -374,9 +448,9 @@
             vmem((NZ, slab * DEPTH, BS), F32),
             vmem((slab, chunk, BS), BF16),
             vmem((slab, chunk, BS), BF16),
-            vmem((slab, NZ, 128), F32),
-            vmem((slab, NZ, 128), F32),
-            vmem((NZ, tall_lanes), F32),
+            vmem((slab, lines, 128), F32),
+            vmem((slab, lines, 128), F32),
+            vmem((lines, tall_lanes), F32),
             vmem((NZ, 8, BS), F32),
             vmem((NZ, 8, BS), F32),
             vmem((NZ, 8, BS), F32),
@@ -387,17 +461,23 @@
             vmem((npoints, 128), jnp.int32),
             dma((n, slab)), dma((n, slab)), dma((slab,)), dma((slab,)), dma((slab,)), dma((slab,)),
             dma((2, 4)), dma((2, 4)), dma((n, 2, 4)), dma((n, 2, 4)),
-            dma((NZ,)), dma((NZ,)), dma((ng,)), dma((ng,)), dma,
+            dma((NZ,)), dma((NZ,)), dma((ng,)), dma((ng,)), dma, dma,
         ],
         compiler_params=pltpu.CompilerParams(
-            collective_id=0, has_side_effects=True, vmem_limit_bytes=67043328
+            collective_id=name, has_side_effects=True, vmem_limit_bytes=67043328
         ),
     )(blocks.reshape(1, npoints), finals[None, :], points, centroids)
 
 
 def shards(points, blocks, finals, centroids):
     dims = tuple(lax.axis_size(a) for a in ("x", "core", "y"))
-    distances, refreshed = fused(blocks, finals, points, centroids, dims)
+    distances, refreshed, flag = fused(blocks, finals, points, centroids, dims, ROOM, 0)
+    if ROOM < NZ * DEPTH:
+        distances, refreshed = lax.cond(
+            flag[0, 0] > 0.5,
+            lambda: fused(blocks, finals, points, centroids, dims, NZ * DEPTH, 1)[:2],
+            lambda: (distances, refreshed),
+        )
     return distances, refreshed.reshape(-1, refreshed.shape[2]).astype(F32)
 
 

time: 167 us -> 160 us (0.958); the launches traced: 164 us -> 160 us
  Pallas kernels: 159 us -> 153 us
    pallas_call x1, Pallas kernels: 159 us -> 153 us  [fused(): pl.pallas_call(functools.partial(kernel, dims, room), out_shape=(jax.Shap...]
where the time goes in v5:
time: 160 us
  Pallas kernels  153 us (96%)
  local copies, waits for them, and re-layouts  3.45 us (2%)
  other arithmetic  2.08 us (1%)
    pallas_call x1, Pallas kernels, fused(): pl.pallas_call(functools.partial(kernel, dims, room), out_shape=(jax.Shap...  153 us

profile of v5, /device:TPU:6, one launch (start us, length us, event | category | flops | bytes accessed | tf_op | source)
XLA Modules:
  0.0 160.0 jit_solution(16804625688543269195)
XLA Ops:
  0.6 153.0 %shard_map.59 = (bf16[2048,256]{1,0:T(8,128)(2,1)}, bf16[8,256,128]{2,1,0:T(8,128)(2,1)}, f32[8,128]{1,0:T(8,128)}) custom-call(s32[1,2048]{1,0:T(1,128)} %bitcast.8, s32[1,2048]{1,0:T(1,128)} %bitcast.10, bf16[2048,1024]{1,0:T(8,128)(2,1)} %points_in.1, bf16[2048,1024]{1,0:T(8,128)(2,1)} %centroids.1), custom_call_target="tpu_custom_call" | custom-call | tf_op jit(solution)/shard_map/pallas_call | solution.py:430
  153.6 1.2 slice.3
  155.5 0.2 conditional.2
  155.7 2.1 %bitcast_convert_fusion = f32[2048,128]{1,0:T(8,128)} fusion(bf16[8,256,128]{2,1,0:T(8,128)(2,1)} %get-tuple-element.40), kind=kLoop, calls=%fused_computation | loop fusion | flops 262144 | bytes 1572864 | tf_op jit(solution)/shard_map/convert_element_type | solution.py:481
  157.8 2.3 %copy.11 = bf16[2048,256]{1,0:T(8,128)(2,1)} copy(bf16[2048,256]{1,0:T(8,128)(2,1)} %get-tuple-element.47) | data formatting | bytes 2097152

commit v6 on v4

--- a/solution.py
+++ b/solution.py
@@ -17,11 +17,11 @@
 
 
 def kernel(
-    dims, blocks_row, finals_row, points, centroids, dist_out, fresh_out,
-    sendbuf, recvbuf, rsend, rrecv, table, sums, partial, dsend, dret, tsend, trecv, tall,
-    csend, crecv, cnorm, denom, fsend, acc, slots_row, slots_col,
+    dims, blocks_row, finals_row, points_in, centroids, dist_out, fresh_out,
+    points, sendbuf, recvbuf, rsend, rrecv, table, sums, partial, dsend, dret, tsend, trecv, tall,
+    csend, crecv, cnorm, denom, fsend, acc, near, slots_row, slots_col,
     p_send, p_recv, t_send, t_recv, d_send, d_recv, g_send, g_recv, r_send, r_recv,
-    c_send, c_recv, f_send, f_recv, local_sem,
+    c_send, c_recv, f_send, f_recv, local_sem, points_sem,
 ):
     nx, nc, ny = dims
     ng = nx * nc
@@ -86,6 +86,8 @@
         centroids.at[pl.ds(pl.multiple_of(g * BS, BS), BS)], table.at[z], local_sem
     )
     own_copy.start()
+    points_copy = pltpu.make_async_copy(points_in, points, points_sem)
+    points_copy.start()
 
     ids = blocks_row[...]
     dest = ((ids & (ng - 1)) * ny + (lax.shift_right_logical(ids, ng.bit_length() - 1) & (ny - 1))) * NZ
@@ -93,11 +95,13 @@
     strip = min(256, npoints)
     earlier = lax.broadcasted_iota(jnp.int32, (strip, strip), 0) < lax.broadcasted_iota(jnp.int32, (strip, strip), 1)
     earlier = jnp.where(earlier, 1.0, 0.0).astype(BF16)
+    strips = [dest[:, q * strip : (q + 1) * strip] for q in range(npoints // strip)]
+    members = [
+        jnp.where(lax.broadcasted_iota(jnp.int32, (slab * NZ, strip), 0) == part, 1.0, 0.0) for part in strips
+    ]
     seen = jnp.zeros((slab * NZ, 1), F32)
     ranks = []
-    for q in range(npoints // strip):
-        part = dest[:, q * strip : (q + 1) * strip]
-        member = jnp.where(lax.broadcasted_iota(jnp.int32, (slab * NZ, strip), 0) == part, 1.0, 0.0)
+    for member in members:
         before = jnp.dot(member.astype(BF16), earlier, preferred_element_type=F32) + seen
         ranks.append(jnp.sum(member * before, axis=0, keepdims=True))
         seen = seen + jnp.sum(member, axis=1, keepdims=True)
@@ -134,6 +138,7 @@
                 ring_copy(way, step, 0).start()
 
     ring_step(0)
+    points_copy.wait()
 
     def dispatch(h):
         def body(i, _):
@@ -183,7 +188,7 @@
 
     def add_up(h):
         def body(j, _):
-            want = tall[pl.ds(j, 1), :][:, :nrow]
+            want = tall[pl.ds(j, 1), :nrow]
             centroid = lax.broadcasted_iota(jnp.int32, (BS, nrow), 0).astype(F32) + 1.0
             hot = jnp.where(want == centroid, 1.0, 0.0).astype(BF16)
             sums[j, :, pieces[h]] = jnp.dot(hot, rows_of(h, j), preferred_element_type=F32)
@@ -280,21 +285,30 @@
 
         return 0
 
-    for h in range(len(pieces)):
+    def arrived(h):
         others(slab, me, lambda s: point_copy(h, s, s).wait_recv())
+
+    last = len(pieces) - 1
+    for h in range(last):
+        arrived(h)
         add_up(h)
         if h == 0:
             others(NZ, z, lambda z2: count_copy(z2, z).start())
         reduce_step(h, 0)
         measure(h)
-        if h == len(pieces) - 1:
-            lax.fori_loop(0, ng, give_back, 0)
-            dret[me] = dsend[me]
-        for step in range(1, 4):
+        for step in range(1, 4 if h < last - 1 else 3):
             reduce_step(h, step)
-        finish(h)
-
-    def bring(i, _):
+        if h < last - 1:
+            finish(h)
+    arrived(last)
+    measure(last)
+    lax.fori_loop(0, ng, give_back, 0)
+    dret[me] = dsend[me]
+    add_up(last)
+    reduce_step(last, 0)
+    reduce_step(last - 1, 3)
+
+    def bring(i):
         dx, dc = offset(i)
         g2 = ((x + nx - dx) % nx) * nc + (c + dc) % nc
         for dy in range(ny):
@@ -318,26 +332,46 @@
         def _():
             acc[...] += part
 
-        return 0
-
-    lax.fori_loop(0, ng, bring, 0)
-    dist_out[...] = acc[...].astype(BF16)
-
-    others(ng, g, lambda g2: fresh_copy(g2, g2).wait_recv())
-    frecv[g] = fsend[g]
-
+    def bring_some(low, high):
+        def body(i, _):
+            bring(i)
+            return 0
+
+        lax.fori_loop(low, high, body, 0)
+
+    def sent(h):
+        others(slab, me, lambda d: point_copy(h, d, me).wait_send())
+
+    sent(0)
+    reduce_step(last, 1)
+    finish(last - 1)
+    bring_some(0, ng // 4)
+    for h in range(1, len(pieces)):
+        sent(h)
+    reduce_step(last, 2)
     others(slab, me, lambda d: target_copy(d, me).wait_send())
-    others(slab, me, lambda d: dist_copy(d, me).wait_send())
     others(NZ, z, lambda z2: count_copy(z2, z).wait_send())
-    others(ng, g, lambda g2: fresh_copy(g2, g).wait_send())
     for way in range(2):
         for step in range(4):
             ring_copy(way, step, 0).wait_send()
+    bring_some(ng // 4, ng // 2)
+    reduce_step(last, 3)
+    bring_some(ng // 2, 3 * ng // 4)
+    finish(last)
     for h in range(len(pieces)):
-        others(slab, me, lambda d: point_copy(h, d, me).wait_send())
         for way in range(2):
             for step in range(4):
                 reduce_copy(h, way, step).wait_send()
+    bring_some(3 * ng // 4, ng)
+    near[...] = acc[...].astype(BF16)
+    out_copy = pltpu.make_async_copy(near, dist_out, points_sem)
+    out_copy.start()
+
+    others(ng, g, lambda g2: fresh_copy(g2, g2).wait_recv())
+    frecv[g] = fsend[g]
+    others(slab, me, lambda d: dist_copy(d, me).wait_send())
+    others(ng, g, lambda g2: fresh_copy(g2, g).wait_send())
+    out_copy.wait()
 
 
 def bounds(width):
@@ -362,9 +396,10 @@
             jax.ShapeDtypeStruct((npoints, BS), BF16),
             jax.ShapeDtypeStruct((ng, BS, share), BF16),
         ),
-        in_specs=[pl.BlockSpec(memory_space=vmem)] * 3 + [pl.BlockSpec(memory_space=pl.ANY)],
-        out_specs=(pl.BlockSpec(memory_space=vmem),) * 2,
+        in_specs=[pl.BlockSpec(memory_space=vmem)] * 2 + [pl.BlockSpec(memory_space=pl.ANY)] * 2,
+        out_specs=(pl.BlockSpec(memory_space=pl.ANY), pl.BlockSpec(memory_space=vmem)),
         scratch_shapes=[
+            vmem((npoints, width), BF16),
             tuple(vmem((slab, chunk, size), BF16) for size in sizes),
             tuple(vmem((slab, chunk, size), BF16) for size in sizes),
             tuple(vmem((2, 4, BS, size), BF16) for size in sizes),
@@ -383,11 +418,12 @@
             vmem((BS, 128), F32),
             vmem((ng, BS, share), BF16),
             vmem((npoints, BS), F32),
+            vmem((npoints, BS), BF16),
             vmem((1, npoints), jnp.int32),
             vmem((npoints, 128), jnp.int32),
             dma((n, slab)), dma((n, slab)), dma((slab,)), dma((slab,)), dma((slab,)), dma((slab,)),
             dma((2, 4)), dma((2, 4)), dma((n, 2, 4)), dma((n, 2, 4)),
-            dma((NZ,)), dma((NZ,)), dma((ng,)), dma((ng,)), dma,
+            dma((NZ,)), dma((NZ,)), dma((ng,)), dma((ng,)), dma, dma,
         ],
         compiler_params=pltpu.CompilerParams(
             collective_id=0, has_side_effects=True, vmem_limit_bytes=67043328

time: 167 us -> 161 us (0.964); the launches traced: 164 us -> 160 us
  Pallas kernels: 159 us -> 155 us
    pallas_call x1, Pallas kernels: 159 us -> 155 us  [fused(): pl.pallas_call(functools.partial(kernel, dims), out_shape=(jax.ShapeDtype...]
where the time goes in v6:
time: 161 us; the launch traced here: 160 us
  Pallas kernels  155 us (96%)
  local copies, waits for them, and re-layouts  2.26 us (1%)
  other arithmetic  2.08 us (1%)
    pallas_call x1, Pallas kernels, fused(): pl.pallas_call(functools.partial(kernel, dims), out_shape=(jax.ShapeDtype...  155 us

profile of v6, /device:TPU:6, one launch (start us, length us, event | category | flops | bytes accessed | tf_op | source)
XLA Modules:
  0.0 159.7 jit_solution(18255318176641632363)
XLA Ops:
  0.6 154.7 %shard_map.59 = (bf16[2048,256]{1,0:T(8,128)(2,1)}, bf16[8,256,128]{2,1,0:T(8,128)(2,1)}) custom-call(s32[1,2048]{1,0:T(1,128)} %bitcast.5, s32[1,2048]{1,0:T(1,128)} %bitcast.6, bf16[2048,1024]{1,0:T(8,128)(2,1)} %points_in.1, bf16[2048,1024]{1,0:T(8,128)(2,1)} %centroids.1), custom_call_target="tpu_custom_call" | custom-call | tf_op jit(solution)/shard_map/pallas_call | solution.py:393
  155.4 2.1 %bitcast_convert_fusion = f32[2048,128]{1,0:T(8,128)} fusion(bf16[8,256,128]{2,1,0:T(8,128)(2,1)} %get-tuple-element.5), kind=kLoop, calls=%fused_computation | loop fusion | flops 262144 | bytes 1572864 | tf_op jit(solution)/shard_map/convert_element_type | solution.py:437
  157.4 2.3 %copy.7 = bf16[2048,256]{1,0:T(8,128)(2,1)} copy(bf16[2048,256]{1,0:T(8,128)(2,1)} %get-tuple-element.8) | data formatting | bytes 2097152

commit v7 on v6

--- a/solution.py
+++ b/solution.py
@@ -74,7 +74,7 @@
         lax.fori_loop(0, n, body, 0)
 
     def offset(i):
-        turn = (2 * (i % nx) + 1) % 5 if nx == 4 else i % nx
+        turn = (2 * ((i + 2 * c) % nx) + 1) % 5 if nx == 4 else i % nx
         return turn, i // nx
 
     barrier = pltpu.get_barrier_semaphore()

time: 161 us -> 155 us (0.963)
  Pallas kernels: 155 us -> 150 us
    pallas_call x1, Pallas kernels: 155 us -> 150 us  [fused(): pl.pallas_call(functools.partial(kernel, dims), out_shape=(jax.ShapeDtype...]
where the time goes in v7:
time: 155 us
  Pallas kernels  150 us (97%)
  local copies, waits for them, and re-layouts  2.26 us (1%)
  other arithmetic  2.08 us (1%)
    pallas_call x1, Pallas kernels, fused(): pl.pallas_call(functools.partial(kernel, dims), out_shape=(jax.ShapeDtype...  150 us

profile of v7, /device:TPU:6, one launch (start us, length us, event | category | flops | bytes accessed | tf_op | source)
XLA Modules:
  0.0 155.2 jit_solution(13158356581812803645)
XLA Ops:
  0.6 150.2 %shard_map.59 = (bf16[2048,256]{1,0:T(8,128)(2,1)}, bf16[8,256,128]{2,1,0:T(8,128)(2,1)}) custom-call(s32[1,2048]{1,0:T(1,128)} %bitcast.5, s32[1,2048]{1,0:T(1,128)} %bitcast.6, bf16[2048,1024]{1,0:T(8,128)(2,1)} %points_in.1, bf16[2048,1024]{1,0:T(8,128)(2,1)} %centroids.1), custom_call_target="tpu_custom_call" | custom-call | tf_op jit(solution)/shard_map/pallas_call | solution.py:393
  150.8 2.1 %bitcast_convert_fusion = f32[2048,128]{1,0:T(8,128)} fusion(bf16[8,256,128]{2,1,0:T(8,128)(2,1)} %get-tuple-element.5), kind=kLoop, calls=%fused_computation | loop fusion | flops 262144 | bytes 1572864 | tf_op jit(solution)/shard_map/convert_element_type | solution.py:437
  152.9 2.3 %copy.7 = bf16[2048,256]{1,0:T(8,128)(2,1)} copy(bf16[2048,256]{1,0:T(8,128)(2,1)} %get-tuple-element.8) | data formatting | bytes 2097152
